TPU v7x, 32 devices: a whole 2x2x4 slice. The times are simulated.
32 devices in a mesh: row: 4 (over y, x), col: 4 (over z), batch: 2 (over core).
Axes of the slice: x: 2, y: 2, z: 4, core: 2. Of those that a mesh axis runs over, the one named last changes fastest.
Arguments:
- item_ids: int32 [4, 4, 2048], P('batch', 'col', 'row'), parts along dimension 0, may hold values from 0 to 511
- pad_masks: int32 [4, 4, 2048], P('batch', 'col', 'row'), parts along dimension 0, may hold values from 0 to 1
- lengths: int32 [4], P('batch'), parts along dimension 0, may hold values from 7168 to 8192
- item_table: bfloat16 [512, 1024], replicated, may hold values from -5 to 5
- w_gate: bfloat16 [1024, 1024], replicated, may hold values from -0.1875 to 0.1875
- w_in: bfloat16 [1024, 1280], replicated, may hold values from -0.1875 to 0.1875
- w_dt: bfloat16 [1024, 8], replicated, may hold values from -0.1875 to 0.1875
- conv_taps: float32 [4, 1280], replicated, may hold values from -3 to 3
- dt_bias: float32 [8], replicated, may hold values from -2 to 1
- decay_rates: float32 [8], replicated, may hold values from 1.2207031e-05 to 0.05
- norm_gain: float32 [1024], replicated, may hold values from 0.1 to 1.9
- w_out: bfloat16 [1024, 1024], replicated, may hold values from -0.1875 to 0.1875
Outputs:
- result: bfloat16 [4, 4, 2048, 1024], P('batch', 'col', 'row'), parts along dimension 0
There are 2 independent parts, one for each index of `batch`. A program takes and returns all parts, laid end to end along the dimension named above; an argument that names none is the same for every part. Nothing has to cross between parts.
Inputs may be any that keep to these rules, and one draw needn't show every extreme that they name: `lengths`: every history keeps at least its first 7168 positions before padding.
All inputs are finite; a program needn't handle non-finite values.
Results may differ from a plain program's by a relative error of at most 0.0093.
Values may be sent and summed in bfloat16 or wider, within the bound.
A program may use at most 128 MiB of HBM per device.

v0:
```python
import functools

import jax
import jax.numpy as jnp
from jax import lax
from jax.experimental import pallas as pl
from jax.experimental.pallas import tpu as pltpu
from jax.sharding import PartitionSpec as P

STRETCH = 128
LANES = 128
HALO = 16
MESH = pl.DeviceIdType.MESH
F32 = jnp.float32
BF16 = jnp.bfloat16


def silu(v):
    return 0.5 * v * (1.0 + jnp.tanh(0.5 * v))


def project_kernel(
    counts,
    mesh_sizes,
    ids_ref,
    table_ref,
    win_ref,
    wgate_ref,
    wdt_ref,
    tin_ref,
    tgate_ref,
    tdt_ref,
    halo_ref,
    wide,
    landed,
    send_sem,
    recv_sem,
):
    rows, cols = mesh_sizes
    r, c = lax.axis_index("row"), lax.axis_index("col")
    place = c * rows + r
    later = lax.rem(place + 1, rows * cols)
    earlier = lax.rem(place + rows * cols - 1, rows * cols)
    after = {"row": lax.rem(later, rows), "col": later // rows}
    ahead = {"row": lax.rem(earlier, rows), "col": earlier // rows}
    has_after, has_before = place < rows * cols - 1, place > 0
    barrier = pltpu.get_barrier_semaphore()
    events = ids_ref.shape[2]
    copy = pltpu.make_async_remote_copy(
        src_ref=ids_ref.at[:, :, pl.ds(events - STRETCH, STRETCH)],
        dst_ref=landed,
        send_sem=send_sem,
        recv_sem=recv_sem,
        device_id=after,
        device_id_type=MESH,
    )
    begin = pl.program_id(0) == 0

    @pl.when(jnp.logical_and(begin, has_before))
    def _():
        pl.semaphore_signal(barrier, inc=1, device_id=ahead, device_id_type=MESH)

    @pl.when(jnp.logical_and(begin, has_after))
    def _():
        pl.semaphore_signal(barrier, inc=1, device_id=after, device_id_type=MESH)

    @pl.when(pl.program_id(0) == 1)
    def _():
        peers = jnp.where(has_before, 1, 0) + jnp.where(has_after, 1, 0)
        pl.semaphore_wait(barrier, peers)

        @pl.when(has_after)
        def _():
            copy.start()

    in_blocks, gate_blocks, head_count = counts
    step = pl.program_id(0)

    @pl.when(step < in_blocks)
    def _():
        tin_ref[...] = jnp.dot(
            table_ref[...], win_ref[...], preferred_element_type=F32
        ).astype(BF16)

    @pl.when(step < gate_blocks)
    def _():
        tgate_ref[...] = jnp.dot(
            table_ref[...], wgate_ref[...], preferred_element_type=F32
        ).astype(BF16)

    @pl.when(step == pl.num_programs(0) - 1)
    def _():
        wide[...] = jnp.zeros_like(wide)
        wide[0:head_count, :] = wdt_ref[...]
        raw = lax.dot_general(
            table_ref[...], wide[...], (((1,), (1,)), ((), ())), preferred_element_type=F32
        )
        high = raw.astype(BF16).astype(F32)
        middle = (raw - high).astype(BF16).astype(F32)
        low = raw - high - middle
        tdt_ref[...] = (
            high + pltpu.roll(middle, head_count, 1) + pltpu.roll(low, 2 * head_count, 1)
        ).astype(BF16)

        @pl.when(has_after)
        def _():
            copy.wait_send()

        @pl.when(has_before)
        def _():
            copy.wait_recv()
            halo_ref[...] = landed[...]

        @pl.when(place == 0)
        def _():
            halo_ref[...] = jnp.full(halo_ref.shape, -1, jnp.int32)


def local_kernel(
    counts,
    lengths_ref,
    ids_ref,
    halo_ref,
    masks_ref,
    tin_ref,
    tgate_ref,
    tdt_ref,
    taps_ref,
    bias_ref,
    rates_ref,
    y_ref,
    gate_ref,
    out_ref,
    ef_ref,
    state_ref,
    log_ref,
    rowbuf,
    partbuf,
    usebuf,
    wide,
    scaled,
    run,
    cum,
):
    stretch_count, head_count, head_size, state_width, pieces = counts
    inner = head_count * head_size
    place = lax.rem(pl.program_id(0), stretch_count)
    user = pl.program_id(0) // stretch_count
    events = stretch_count * STRETCH

    @pl.when(place == 0)
    def _():
        run[...] = jnp.zeros_like(run)
        cum[...] = jnp.zeros_like(cum)
        wide[...] = jnp.zeros_like(wide)
        wide[0:1, 0:head_count] = bias_ref[...]
        wide[1:2, 0:head_count] = rates_ref[...]
        first = (lax.axis_index("col") * pieces + lax.axis_index("row")) * events
        halo = jnp.where(first == 0, -1, halo_ref[0])
        names = jnp.concatenate([halo, ids_ref[0]], axis=1).astype(F32)
        position = first + lax.broadcasted_iota(jnp.int32, (1, events), 1)
        kept = jnp.where(position < lengths_ref[user], masks_ref[0], 0)
        kept = jnp.where(kept > 0, 1.0, 0.0).astype(F32)
        flags = jnp.concatenate([jnp.zeros((1, STRETCH), F32), kept], axis=1)
        line = lax.broadcasted_iota(jnp.int32, (8, STRETCH + events), 0)
        meta = jnp.transpose(jnp.where(line == 0, names, jnp.where(line == 1, flags, 0.0)))
        usebuf[...] = meta[STRETCH:, :]
        ids = meta[STRETCH - HALO :, 0:1].astype(jnp.int32)
        items = tin_ref.shape[0]
        lane = lax.broadcasted_iota(jnp.int32, (HALO + events, items), 1)
        hot = (ids == lane).astype(F32).astype(BF16)
        rowbuf[...] = jnp.dot(hot, tin_ref[...], preferred_element_type=F32)
        now = hot[HALO:]
        gate_ref[...] = jnp.dot(now, tgate_ref[...], preferred_element_type=F32).astype(BF16)
        partbuf[...] = jnp.dot(now, tdt_ref[...], preferred_element_type=F32)

    base = pl.multiple_of(place * STRETCH, STRETCH)
    usable = usebuf[pl.ds(base, STRETCH), :][:, 1:2]
    parts = partbuf[pl.ds(base, STRETCH), :]
    raw = (
        parts
        + pltpu.roll(parts, LANES - head_count, 1)
        + pltpu.roll(parts, LANES - 2 * head_count, 1)
    )
    raw = raw + wide[0:1, :]
    step = usable * (jnp.maximum(raw, 0.0) + jnp.log1p(jnp.exp(-jnp.abs(raw))))
    rows = lax.broadcasted_iota(jnp.int32, (STRETCH, STRETCH), 0)
    cols = lax.broadcasted_iota(jnp.int32, (STRETCH, STRETCH), 1)
    causal = rows >= cols
    logs = jnp.dot(
        jnp.where(causal, 1.0, 0.0).astype(F32),
        step * wide[1:2, :],
        precision=lax.Precision.HIGHEST,
        preferred_element_type=F32,
    )
    total = logs[STRETCH - 1 :, :]
    logs_t = jnp.transpose(logs)
    step_t = jnp.transpose(step)
    kernel = taps_ref.shape[0]
    window = rowbuf[pl.ds(base, HALO + STRETCH), :]
    conv = window * taps_ref[0:1, :]
    for k in range(1, kernel):
        conv = pltpu.roll(conv, 1, 0) + window * taps_ref[k : k + 1, :]
    conv = conv[HALO:, :]
    signal = silu(conv[:, :inner]).astype(BF16)
    inward = conv[:, inner : inner + state_width].astype(BF16)
    outward = conv[:, inner + state_width :].astype(BF16)
    out_ref[...] = outward
    scores = lax.dot_general(
        outward, inward, (((1,), (1,)), ((), ())), preferred_element_type=F32
    )
    scores = jnp.where(causal, scores, 0.0)
    tail = jnp.exp(logs - total) * step
    fade = jnp.exp(-logs)
    held = jnp.dot(outward, run[...].astype(BF16), preferred_element_type=F32)
    for h in range(head_count):
        span = slice(h * head_size, (h + 1) * head_size)
        gap = jnp.minimum(logs_t[h : h + 1, :] - logs[:, h : h + 1], 0.0)
        weights = (jnp.exp(gap) * (scores * step_t[h : h + 1, :])).astype(BF16)
        near = jnp.dot(weights, signal[:, span], preferred_element_type=F32)
        y_ref[:, span] = (near + held[:, span] * fade[:, h : h + 1]).astype(BF16)
        scaled[:, span] = (signal[:, span].astype(F32) * tail[:, h : h + 1]).astype(BF16)
    added = lax.dot_general(
        inward, scaled[...], (((0,), (0,)), ((), ())), preferred_element_type=F32
    )
    shrink = jnp.exp(-total)
    for h in range(head_count):
        span = slice(h * head_size, (h + 1) * head_size)
        run[:, span] = run[:, span] * shrink[:, h : h + 1] + added[:, span]
    before = cum[0:1, :]
    lane = lax.broadcasted_iota(jnp.int32, (STRETCH, LANES), 1)
    ef_ref[...] = jnp.where(lane == LANES - 1, usable, jnp.exp(-(logs + before)))
    after = before + total
    cum[...] = jnp.broadcast_to(after, cum.shape)

    @pl.when(place == stretch_count - 1)
    def _():
        width = inner // pieces
        for q in range(pieces):
            state_ref[q, 0] = run[:, q * width : (q + 1) * width].astype(BF16)
            for j in range(width // head_size):
                h = q * (width // head_size) + j
                log_ref[q, 0, :, j * head_size : (j + 1) * head_size] = jnp.broadcast_to(
                    after[:, h : h + 1], (8, head_size)
                )


def chain_kernel(
    rows,
    cols,
    state_ref,
    log_ref,
    enter_ref,
    rin,
    lin,
    before,
    fades,
    pin,
    psend,
    esend,
    s1,
    r1,
    sl,
    rl,
    s2,
    r2,
    s3,
    r3,
):
    users = state_ref.shape[1]
    r, c = lax.axis_index("row"), lax.axis_index("col")
    barrier = pltpu.get_barrier_semaphore()
    for d in range(1, rows):
        pl.semaphore_signal(
            barrier, inc=1, device_id={"row": lax.rem(r + d, rows)}, device_id_type=MESH
        )

    @pl.when(c > 0)
    def _():
        pl.semaphore_signal(barrier, inc=1, device_id={"col": c - 1}, device_id_type=MESH)

    @pl.when(c < cols - 1)
    def _():
        pl.semaphore_signal(barrier, inc=1, device_id={"col": c + 1}, device_id_type=MESH)

    peers = rows - 1 + jnp.where(c > 0, 1, 0) + jnp.where(c < cols - 1, 1, 0)
    pl.semaphore_wait(barrier, peers)

    first = [[] for _ in range(users)]
    for u in range(users):
        for d in range(1, rows):
            q = lax.rem(r + d, rows)
            for source, target, send, recv in (
                (log_ref, lin, sl, rl),
                (state_ref, rin, s1, r1),
            ):
                copy = pltpu.make_async_remote_copy(
                    src_ref=source.at[q, u],
                    dst_ref=target.at[r, u],
                    send_sem=send.at[d, u],
                    recv_sem=recv.at[d, u],
                    device_id={"row": q},
                    device_id_type=MESH,
                )
                copy.start()
                first[u].append(copy)
    rin[r] = state_ref[r]
    lin[r] = log_ref[r]
    onward = [
        pltpu.make_async_remote_copy(
            src_ref=psend.at[u],
            dst_ref=pin.at[u],
            send_sem=s2.at[u],
            recv_sem=r2.at[u],
            device_id={"col": lax.rem(c + 1, cols)},
            device_id_type=MESH,
        )
        for u in range(users)
    ]

    for u in range(users):
        for copy in first[u]:
            copy.wait_recv()
        carried = jnp.zeros(pin.shape[1:], F32)
        fade = jnp.ones((1, pin.shape[2]), F32)
        for m in range(rows):
            before[m, u] = carried
            fades[m, u] = jnp.broadcast_to(fade, fades.shape[2:])
            here = jnp.exp(-lin[m, u, 0:1, :])
            carried = here * carried + rin[m, u].astype(F32)
            fade = fade * here
        before[rows, u] = carried
        fades[rows, u] = jnp.broadcast_to(fade, fades.shape[2:])
        if cols > 1:

            @pl.when(c == 0)
            def _(u=u, carried=carried):
                psend[u] = carried.astype(BF16)
                onward[u].start()

    @pl.when(c == 0)
    def _():
        pin[...] = jnp.zeros_like(pin)

    third = []
    for u in range(users):

        @pl.when(c > 0)
        def _(u=u):
            onward[u].wait_recv()

        @pl.when(jnp.logical_and(c > 0, c < cols - 1))
        def _(u=u):
            psend[u] = (fades[rows, u, 0:1, :] * pin[u].astype(F32) + before[rows, u]).astype(BF16)
            onward[u].start()

        for d in range(1, rows):
            q = lax.rem(r + d, rows)
            esend[d, u] = (fades[q, u, 0:1, :] * pin[u].astype(F32) + before[q, u]).astype(BF16)
            copy = pltpu.make_async_remote_copy(
                src_ref=esend.at[d, u],
                dst_ref=enter_ref.at[r, u],
                send_sem=s3.at[d, u],
                recv_sem=r3.at[d, u],
                device_id={"row": q},
                device_id_type=MESH,
            )
            copy.start()
            third.append(copy)
        enter_ref[r, u] = (fades[r, u, 0:1, :] * pin[u].astype(F32) + before[r, u]).astype(BF16)
    for copy in third:
        copy.wait()
    for group in first:
        for copy in group:
            copy.wait_send()

    @pl.when(c < cols - 1)
    def _():
        for copy in onward:
            copy.wait_send()


def finish_kernel(
    head_count, y_ref, gate_ref, outward_ref, ef_ref, enter_ref, gain_ref, wout_ref, result_ref, mix
):
    pieces, _, _, width = enter_ref.shape
    inner = pieces * width
    head_size = inner // head_count
    squares = None
    for q in range(pieces):
        far = jnp.dot(outward_ref[...], enter_ref[q, 0], preferred_element_type=F32)
        for j in range(width // head_size):
            h = q * (width // head_size) + j
            span = slice(h * head_size, (h + 1) * head_size)
            both = y_ref[:, span].astype(F32) + far[:, j * head_size : (j + 1) * head_size] * ef_ref[:, h : h + 1]
            value = both * silu(gate_ref[:, span].astype(F32))
            mix[:, span] = value
            squares = value * value if squares is None else squares + value * value
    mean = jnp.sum(squares, axis=1, keepdims=True) * (1.0 / inner)
    normed = (mix[...] * lax.rsqrt(mean + 1.0) * gain_ref[...]).astype(BF16)
    result = jnp.dot(normed, wout_ref[...], preferred_element_type=F32)
    result_ref[...] = (result * ef_ref[:, LANES - 1 : LANES]).astype(BF16)


def per_device(
    item_ids,
    pad_masks,
    lengths,
    item_table,
    w_gate,
    w_in,
    w_dt,
    conv_taps,
    dt_bias,
    decay_rates,
    norm_gain,
    w_out,
):
    users = item_ids.shape[0]
    events = item_ids.shape[2]
    items, model = item_table.shape
    full_width = w_in.shape[1]
    inner = w_gate.shape[1]
    head_count = decay_rates.shape[0]
    head_size = inner // head_count
    state_width = (full_width - inner) // 2
    rows, cols = lax.axis_size("row"), lax.axis_size("col")
    stretch_count = events // STRETCH
    steps = users * stretch_count
    width = inner // rows

    def whole(shape):
        return pl.BlockSpec(shape, lambda s: (0,) * len(shape))

    def by_rows(columns):
        return pl.BlockSpec((STRETCH, columns), lambda s: (s, 0))

    total_rows = users * events
    block = 2 * LANES
    in_blocks, gate_blocks = full_width // block, inner // block
    table_in, table_gate, table_dt, halo = pl.pallas_call(
        functools.partial(project_kernel, (in_blocks, gate_blocks, head_count), (rows, cols)),
        grid=(max(in_blocks, gate_blocks),),
        in_specs=[
            whole(item_ids.shape),
            whole((items, model)),
            pl.BlockSpec((model, block), lambda s: (0, jnp.minimum(s, in_blocks - 1))),
            pl.BlockSpec((model, block), lambda s: (0, jnp.minimum(s, gate_blocks - 1))),
            whole(w_dt.shape[::-1]),
        ],
        out_specs=[
            pl.BlockSpec((items, block), lambda s: (0, jnp.minimum(s, in_blocks - 1))),
            pl.BlockSpec((items, block), lambda s: (0, jnp.minimum(s, gate_blocks - 1))),
            whole((items, LANES)),
            whole((users, 1, STRETCH)),
        ],
        out_shape=[
            jax.ShapeDtypeStruct((items, full_width), BF16),
            jax.ShapeDtypeStruct((items, inner), BF16),
            jax.ShapeDtypeStruct((items, LANES), BF16),
            jax.ShapeDtypeStruct((users, 1, STRETCH), jnp.int32),
        ],
        scratch_shapes=[
            pltpu.VMEM((LANES, model), BF16),
            pltpu.VMEM((users, 1, STRETCH), jnp.int32),
            pltpu.SemaphoreType.DMA,
            pltpu.SemaphoreType.DMA,
        ],
        compiler_params=pltpu.CompilerParams(
            dimension_semantics=("arbitrary",), collective_id=1, has_side_effects=True
        ),
        cost_estimate=pl.CostEstimate(
            flops=2 * items * model * (full_width + inner),
            bytes_accessed=4 * model * (full_width + inner),
            transcendentals=0,
        ),
        name="table_part",
    )(item_ids, item_table, w_in, w_gate, w_dt.T)

    def by_user(columns):
        return pl.BlockSpec((1, 1, columns), lambda s: (s // stretch_count, 0, 0))

    y, gate, outward, ef, state, logs = pl.pallas_call(
        functools.partial(
            local_kernel, (stretch_count, head_count, head_size, state_width, rows)
        ),
        grid=(steps,),
        in_specs=[
            pl.BlockSpec(memory_space=pltpu.SMEM),
            by_user(events),
            by_user(STRETCH),
            by_user(events),
            whole((items, full_width)),
            whole((items, inner)),
            whole((items, LANES)),
            whole(conv_taps.shape),
            whole((1, head_count)),
            whole((1, head_count)),
        ],
        out_specs=[
            by_rows(inner),
            pl.BlockSpec((events, inner), lambda s: (s // stretch_count, 0)),
            by_rows(state_width),
            by_rows(LANES),
            pl.BlockSpec((rows, 1, state_width, width), lambda s: (0, s // stretch_count, 0, 0)),
            pl.BlockSpec((rows, 1, 8, width), lambda s: (0, s // stretch_count, 0, 0)),
        ],
        out_shape=[
            jax.ShapeDtypeStruct((total_rows, inner), BF16),
            jax.ShapeDtypeStruct((total_rows, inner), BF16),
            jax.ShapeDtypeStruct((total_rows, state_width), BF16),
            jax.ShapeDtypeStruct((total_rows, LANES), F32),
            jax.ShapeDtypeStruct((rows, users, state_width, width), BF16),
            jax.ShapeDtypeStruct((rows, users, 8, width), F32),
        ],
        scratch_shapes=[
            pltpu.VMEM((HALO + events, full_width), F32),
            pltpu.VMEM((events, LANES), F32),
            pltpu.VMEM((events, 8), F32),
            pltpu.VMEM((8, LANES), F32),
            pltpu.VMEM((STRETCH, inner), BF16),
            pltpu.VMEM((state_width, inner), F32),
            pltpu.VMEM((8, LANES), F32),
        ],
        compiler_params=pltpu.CompilerParams(dimension_semantics=("arbitrary",)),
        name="local_part",
    )(
        lengths,
        item_ids,
        halo,
        pad_masks,
        table_in,
        table_gate,
        table_dt,
        conv_taps,
        dt_bias[None],
        decay_rates[None],
    )

    vmem = pl.BlockSpec(memory_space=pltpu.VMEM)
    dma = pltpu.SemaphoreType.DMA
    entering = pl.pallas_call(
        functools.partial(chain_kernel, rows, cols),
        in_specs=[vmem, vmem],
        out_specs=vmem,
        out_shape=jax.ShapeDtypeStruct(state.shape, BF16),
        scratch_shapes=[
            pltpu.VMEM(state.shape, BF16),
            pltpu.VMEM(logs.shape, F32),
            pltpu.VMEM((rows + 1,) + state.shape[1:], F32),
            pltpu.VMEM((rows + 1,) + logs.shape[1:], F32),
            pltpu.VMEM(state.shape[1:], BF16),
            pltpu.VMEM(state.shape[1:], BF16),
            pltpu.VMEM(state.shape, BF16),
            dma((rows, users)),
            dma((rows, users)),
            dma((rows, users)),
            dma((rows, users)),
            dma((users,)),
            dma((users,)),
            dma((rows, users)),
            dma((rows, users)),
        ],
        compiler_params=pltpu.CompilerParams(collective_id=0, has_side_effects=True),
        name="state_chain",
    )(state, logs)

    tall = 2 * STRETCH if events % (2 * STRETCH) == 0 else STRETCH

    def tall_rows(columns):
        return pl.BlockSpec((tall, columns), lambda s: (s, 0))

    result = pl.pallas_call(
        functools.partial(finish_kernel, head_count),
        grid=(total_rows // tall,),
        in_specs=[
            tall_rows(inner),
            tall_rows(inner),
            tall_rows(state_width),
            tall_rows(LANES),
            pl.BlockSpec((rows, 1, state_width, width), lambda s: (0, s // (events // tall), 0, 0)),
            whole((1, inner)),
            whole(w_out.shape),
        ],
        out_specs=tall_rows(w_out.shape[1]),
        out_shape=jax.ShapeDtypeStruct((total_rows, w_out.shape[1]), BF16),
        scratch_shapes=[pltpu.VMEM((tall, inner), F32)],
        compiler_params=pltpu.CompilerParams(dimension_semantics=("arbitrary",)),
        name="finish_part",
    )(y, gate, outward, ef, entering, norm_gain[None], w_out)
    return result.reshape(users, 1, events, -1)


def solution(mesh):
    in_specs = (
        P("batch", "col", "row"),
        P("batch", "col", "row"),
        P("batch"),
        P(),
        P(),
        P(),
        P(),
        P(),
        P(),
        P(),
        P(),
        P(),
    )
    out_specs = P("batch", "col", "row", None)
    return jax.shard_map(
        per_device, mesh=mesh, in_specs=in_specs, out_specs=out_specs, check_vma=False
    )
```

profile of v0, /device:TPU:24, one launch (start us, length us, event | category | flops | bytes accessed | tf_op | source)
XLA Modules:
  0.0 61.1 jit_solution(285058290990596040)
XLA Ops:
  0.0 9.1 %table_part.1 = (bf16[512,1280]{1,0:T(8,128)(2,1)}, bf16[512,1024]{1,0:T(8,128)(2,1)}, bf16[512,128]{1,0:T(8,128)(2,1)}, s32[2,1,128]{2,1,0:T(1,128)}) custom-call(s32[2,1,512]{2,1,0:T(1,128)} %ids_ref.3, bf16[512,1024]{1,0:T(8,128)(2,1)} %table_ref.1, bf16[1024,1280]{1,0:T(8,128)(2,1)} %win_ref.1, bf16[1024,1024]{1,0:T(8,128)(2,1)} %wgate_ref.1, ...), custom_call_target="tpu_custom_call" | custom-call | flops 2415919104 | bytes 9437184 | tf_op jit(solution)/shard_map/table_part/pallas_call | solution.py:441
  9.1 18.1 %local_part.1 = (bf16[1024,1024]{1,0:T(8,128)(2,1)}, bf16[1024,1024]{1,0:T(8,128)(2,1)}, bf16[1024,128]{1,0:T(8,128)(2,1)}, f32[1024,128]{1,0:T(8,128)}, bf16[4,...) custom-call(s32[2]{0:T(128)} %lengths_ref.1, s32[2,1,512]{2,1,0:T(1,128)} %ids_ref.3, ...), custom_call_target="tpu_custom_call" | custom-call | tf_op jit(solution)/shard_map/local_part/pallas_call | solution.py:483
  27.2 24.0 %state_chain.1.enter_ref = bf16[4,2,128,256]{3,2,1,0:T(8,128)(2,1)} custom-call(bf16[4,2,128,256]{3,2,1,0:T(8,128)(2,1)} %get-tuple-element.23.state_ref, f32[4,2,8,256]{3,2,1,0:T(8,128)} %get-tuple-element.24.log_ref), custom_call_target="tpu_custom_call" | custom-call | tf_op jit(solution)/shard_map/state_chain/pallas_call | solution.py:542
  51.2 9.9 %finish_part.1 = bf16[1024,1024]{1,0:T(8,128)(2,1)} custom-call(bf16[1024,1024]{1,0:T(8,128)(2,1)} %get-tuple-element.19.y_ref, bf16[1024,1024]{1,0:T(8,128)(2,1)} %get-tuple-element.20.gate_ref, bf16[1024,128]{1,0:T(8,128)(2,1)} %get-tuple-element.21.outward_ref, f32[1024,128]{1,0:T(8,128)} %get-tuple-element.22.ef_ref, ...), custom_call_target="tpu_custom_call" | custom-call | tf_op jit(solution)/shard_map/finish_part/pallas_call | solution.py:573
where the time goes:
time: 61.4 us; the launch traced here: 61.1 us
  Pallas kernels  61.1 us (100%)
    pallas_call x1, Pallas kernels, per_device(): pl.pallas_call(functools.partial(chain_kernel, rows, cols), in_specs=[vme...  24 us
    pallas_call x1, Pallas kernels, per_device(): pl.pallas_call(functools.partial(local_kernel, (stretch_count, head_count...  18.1 us
    pallas_call x1, Pallas kernels, per_device(): pl.pallas_call(functools.partial(finish_kernel, head_count), grid=(total_...  9.91 us
    pallas_call x1, Pallas kernels, per_device(): pl.pallas_call(functools.partial(project_kernel, (in_blocks, gate_blocks,...  9.1 us

commit v1 on v0

v1 whole, which is shorter than its diff:
```python
import functools

import jax
import jax.numpy as jnp
from jax import lax
from jax.experimental import pallas as pl
from jax.experimental.pallas import tpu as pltpu
from jax.sharding import PartitionSpec as P

STRETCH = 128
LANES = 128
HALO = 16
MESH = pl.DeviceIdType.MESH
F32 = jnp.float32
BF16 = jnp.bfloat16


def silu(v):
    return 0.5 * v * (1.0 + jnp.tanh(0.5 * v))


def remote(src, dst, send, recv, device):
    return pltpu.make_async_remote_copy(
        src_ref=src,
        dst_ref=dst,
        send_sem=send,
        recv_sem=recv,
        device_id=device,
        device_id_type=MESH,
    )


def mixer_kernel(
    counts,
    lengths_ref,
    ids_ref,
    masks_ref,
    wdt_ref,
    taps_ref,
    bias_ref,
    rates_ref,
    gain_ref,
    table_hbm,
    win_hbm,
    wgate_hbm,
    wout_hbm,
    out_ref,
    table,
    win,
    wgate,
    wout,
    tin,
    tgate,
    tdt,
    wide,
    params,
    ptaps,
    hot,
    rowbuf,
    inward_t,
    outward,
    logs,
    logs_t,
    steps_t,
    tails,
    shrinks,
    ef,
    signal,
    scaled,
    held,
    ssend,
    rin,
    aft,
    lin,
    before,
    pin,
    psend,
    esend,
    enter,
    y,
    gates,
    mix,
    ostage,
    landed,
    wsem,
    osem,
    hsem,
    ssem,
    lsem_s,
    lsem_r,
    s1,
    r1,
    s2,
    r2,
    s3,
    r3,
):
    rows, cols, users, heads, tall = counts
    events = ids_ref.shape[2]
    stretches = events // STRETCH
    kernel = taps_ref.shape[0]
    inner = wgate.shape[1]
    per = heads // rows
    pieces = users * per
    wide_group = rows * LANES
    r, c = lax.axis_index("row"), lax.axis_index("col")
    place = c * rows + r
    places = rows * cols
    later = lax.rem(place + 1, places)
    earlier = lax.rem(place + places - 1, places)
    after = {"row": lax.rem(later, rows), "col": later // rows}
    ahead = {"row": lax.rem(earlier, rows), "col": earlier // rows}
    has_after, has_before = place < places - 1, place > 0
    wraps = jnp.logical_and(r == rows - 1, c < cols - 1)
    wrapped = jnp.logical_and(r == 0, c > 0)

    def head_of(p):
        return (p % rows) * per + p // rows

    def column(p):
        source = p if p >= heads else head_of(p)
        return pltpu.make_async_copy(
            win_hbm.at[:, pl.ds(source * LANES, LANES)],
            win.at[:, pl.ds(p * LANES, LANES)],
            wsem.at[p],
        )

    blocks = heads + 2
    table_copy = pltpu.make_async_copy(table_hbm, table, wsem.at[blocks])
    wgate_copy = pltpu.make_async_copy(wgate_hbm, wgate, wsem.at[blocks + 1])
    wout_copy = pltpu.make_async_copy(wout_hbm, wout, wsem.at[blocks + 2])
    table_copy.start()
    for p in (heads, heads + 1, *range(heads)):
        column(p).start()
    wgate_copy.start()
    wout_copy.start()

    barrier = pltpu.get_barrier_semaphore()
    for d in range(1, rows):
        pl.semaphore_signal(
            barrier, inc=1, device_id={"row": lax.rem(r + d, rows)}, device_id_type=MESH
        )

    @pl.when(c > 0)
    def _():
        pl.semaphore_signal(barrier, inc=1, device_id={"col": c - 1}, device_id_type=MESH)

    @pl.when(c < cols - 1)
    def _():
        pl.semaphore_signal(barrier, inc=1, device_id={"col": c + 1}, device_id_type=MESH)

    @pl.when(wraps)
    def _():
        pl.semaphore_signal(barrier, inc=1, device_id=after, device_id_type=MESH)

    @pl.when(wrapped)
    def _():
        pl.semaphore_signal(barrier, inc=1, device_id=ahead, device_id_type=MESH)

    halo_copy = remote(
        ids_ref.at[:, :, pl.ds(events - STRETCH, STRETCH)], landed, hsem.at[0], hsem.at[1], after
    )

    params[...] = jnp.zeros_like(params)
    wide[...] = jnp.zeros_like(wide)
    for p in range(heads):
        h = head_of(p)
        params[0:1, p : p + 1] = bias_ref[:, h : h + 1]
        params[1:2, p : p + 1] = rates_ref[:, h : h + 1]
    wide[0:heads, :] = jnp.concatenate(
        [wdt_ref[head_of(p) : head_of(p) + 1, :] for p in range(heads)], axis=0
    )
    for p in range(blocks):
        source = p if p >= heads else head_of(p)
        ptaps[p, 0:kernel, :] = taps_ref[:, source * LANES : (source + 1) * LANES]

    table_copy.wait()

    def table_block(first):
        span = pl.ds(first, 2 * LANES)
        if not isinstance(first, int):
            span = pl.ds(pl.multiple_of(first, 2 * LANES), 2 * LANES)
        tin[:, span] = jnp.dot(table[...], win[:, span], preferred_element_type=F32).astype(BF16)

    column(heads).wait()
    column(heads + 1).wait()
    table_block(heads * LANES)

    peers = (
        rows
        - 1
        + jnp.where(c > 0, 1, 0)
        + jnp.where(c < cols - 1, 1, 0)
        + jnp.where(wraps, 1, 0)
        + jnp.where(wrapped, 1, 0)
    )
    pl.semaphore_wait(barrier, peers)

    @pl.when(has_after)
    def _():
        halo_copy.start()

    raw = lax.dot_general(
        table[...], wide[...], (((1,), (1,)), ((), ())), preferred_element_type=F32
    )
    high = raw.astype(BF16).astype(F32)
    middle = (raw - high).astype(BF16).astype(F32)
    low = raw - high - middle
    tdt[...] = (high + pltpu.roll(middle, heads, 1) + pltpu.roll(low, 2 * heads, 1)).astype(BF16)

    for p in range(heads):
        column(p).wait()

    def table_step(i, carry):
        table_block(i * 2 * LANES)
        return carry

    lax.fori_loop(0, heads // 2, table_step, 0)

    @pl.when(place == 0)
    def _():
        landed[...] = jnp.full(landed.shape, -1, jnp.int32)

    @pl.when(has_before)
    def _():
        halo_copy.wait_recv()

    line_rows = lax.broadcasted_iota(jnp.int32, (STRETCH, STRETCH), 0)
    line_cols = lax.broadcasted_iota(jnp.int32, (STRETCH, STRETCH), 1)
    causal = line_rows >= line_cols

    def convolve(position, slot):
        total = None
        for k in range(kernel):
            part = rowbuf[slot, pl.ds(HALO - kernel + 1 + k, events), :] * ptaps[position, k : k + 1, :]
            total = part if total is None else total + part
        return total

    def log_copy(u, d):
        q = lax.rem(r + d, rows)
        return remote(
            aft.at[u, q], lin.at[u, r], lsem_s.at[u, d], lsem_r.at[u, d], {"row": q}
        )

    def state_copy(k, d):
        q = lax.rem(r + d, rows)
        return remote(ssend.at[k, q], rin.at[k, r], s1.at[k, d], r1.at[k, d], {"row": q})

    def onward_copy(k):
        return remote(
            psend.at[k], pin.at[k], s2.at[k], r2.at[k], {"col": lax.rem(c + 1, cols)}
        )

    def enter_copy(k, d):
        q = lax.rem(r + d, rows)
        return remote(esend.at[k, q], enter.at[k, r], s3.at[k, d], r3.at[k, d], {"row": q})

    def prepare(u):
        first = place * events
        names = jnp.concatenate([landed[u], ids_ref[u]], axis=1).astype(F32)
        position = first + lax.broadcasted_iota(jnp.int32, (1, events), 1)
        kept = jnp.where(position < lengths_ref[u], masks_ref[u], 0)
        kept = jnp.where(kept > 0, 1.0, 0.0).astype(F32)
        flags = jnp.concatenate([jnp.zeros((1, STRETCH), F32), kept], axis=1)
        line = lax.broadcasted_iota(jnp.int32, (8, STRETCH + events), 0)
        meta = jnp.transpose(jnp.where(line == 0, names, jnp.where(line == 1, flags, 0.0)))
        usable = meta[STRETCH:, 1:2]
        ids = meta[STRETCH - HALO :, 0:1].astype(jnp.int32)
        items = table.shape[0]
        lane = lax.broadcasted_iota(jnp.int32, (HALO + events, items), 1)
        hot[u] = (ids == lane).astype(F32).astype(BF16)
        both = jnp.dot(hot[u], tin[:, heads * LANES :], preferred_element_type=F32)
        rowbuf[0] = both[:, :LANES]
        rowbuf[1] = both[:, LANES:]
        parts = jnp.dot(hot[u, pl.ds(HALO, events), :], tdt[...], preferred_element_type=F32)
        raw = (
            parts
            + pltpu.roll(parts, LANES - heads, 1)
            + pltpu.roll(parts, LANES - 2 * heads, 1)
        )
        raw = raw + params[0:1, :]
        step = usable * (jnp.maximum(raw, 0.0) + jnp.log1p(jnp.exp(-jnp.abs(raw))))
        paced = step * params[1:2, :]
        inward_t[u] = jnp.transpose(convolve(heads, 0)).astype(BF16)
        outward[pl.ds(pl.multiple_of(u * events, events), events), :] = convolve(heads + 1, 1).astype(BF16)
        past = jnp.zeros((1, LANES), F32)
        lower = jnp.where(causal, 1.0, 0.0).astype(F32)
        for s in range(stretches):
            span = slice(s * STRETCH, (s + 1) * STRETCH)
            log = jnp.dot(
                lower, paced[span], precision=lax.Precision.HIGHEST, preferred_element_type=F32
            )
            logs[u, span, :] = log
            logs_t[u, s] = jnp.transpose(log)[0:8, :]
            steps_t[u, s] = jnp.transpose(step[span])[0:8, :]
            total = log[STRETCH - 1 :, :]
            tail = jnp.exp(log - total) * step[span]
            shrink = jnp.exp(-total)
            for j in range(per):
                turned = tail if j == 0 else pltpu.roll(tail, LANES - j * rows, 1)
                tails[u * per + j, span, :] = turned
                for q in range(rows):
                    p = j * rows + q
                    shrinks[u * per + j, s, :, q * LANES : (q + 1) * LANES] = jnp.broadcast_to(
                        shrink[:, p : p + 1], (8, LANES)
                    )
            lane = lax.broadcasted_iota(jnp.int32, (STRETCH, LANES), 1)
            ef[pl.ds(pl.multiple_of(u * events + s * STRETCH, STRETCH), STRETCH), :] = jnp.where(
                lane == LANES - 1, usable[span], jnp.exp(-(log + past))
            )
            past = past + total
        for q in range(rows):
            for j in range(per):
                p = j * rows + q
                aft[u, q, j] = jnp.broadcast_to(past[:, p : p + 1], (8, LANES))
        for d in range(1, rows):
            log_copy(u, d).start()
        lin[u, r] = aft[u, r]

    def group(u, j):
        k = u * per + j
        base = pl.multiple_of(j * wide_group, wide_group)
        gathered = jnp.dot(hot[u], tin[:, pl.ds(base, wide_group)], preferred_element_type=F32)
        for q in range(rows):
            rowbuf[q] = gathered[:, q * LANES : (q + 1) * LANES]
        for q in range(rows):
            span = slice(q * LANES, (q + 1) * LANES)
            value = silu(convolve(j * rows + q, q)).astype(BF16)
            signal[u, j * rows + q] = value
            scaled[:, span] = (value.astype(F32) * tails[k, :, q : q + 1]).astype(BF16)
        run = None
        for s in range(stretches):
            span = slice(s * STRETCH, (s + 1) * STRETCH)
            added = jnp.dot(
                inward_t[u, :, span], scaled[span, :], preferred_element_type=F32
            )
            if run is None:
                held[k, s] = jnp.zeros_like(held[k, s])
                run = added
            else:
                held[k, s] = run.astype(BF16)
                run = run * shrinks[k, s, 0:1, :] + added
        for q in range(rows):
            ssend[k, q] = run[:, q * LANES : (q + 1) * LANES].astype(BF16)
        for d in range(1, rows):
            state_copy(k, d).start()

    def user_step(u, carry):
        prepare(u)

        def group_step(j, inner_carry):
            group(u, j)
            return inner_carry

        return lax.fori_loop(0, per, group_step, carry)

    lax.fori_loop(0, users, user_step, 0)

    def handle(k, carry):
        u, j = k // per, lax.rem(k, per)
        rin[k, r] = ssend[k, r]

        @pl.when(j == 0)
        def _():
            for d in range(1, rows):
                log_copy(u, d).wait_recv()

        for d in range(1, rows):
            state_copy(k, d).wait_recv()
        carried = jnp.zeros(pin.shape[1:], F32)
        fade = jnp.ones((1, LANES), F32)
        fades = []
        for m in range(rows):
            before[m] = carried
            fades.append(fade)
            here = jnp.exp(-lin[u, m, j, 0:1, :])
            carried = here * carried + rin[k, m].astype(F32)
            fade = fade * here

        @pl.when(c == 0)
        def _():
            pin[k] = jnp.zeros(pin.shape[1:], BF16)
            psend[k] = carried.astype(BF16)
            if cols > 1:
                onward_copy(k).start()

        if cols > 1:

            @pl.when(c > 0)
            def _():
                onward_copy(k).wait_recv()

            @pl.when(jnp.logical_and(c > 0, c < cols - 1))
            def _():
                psend[k] = (fade * pin[k].astype(F32) + carried).astype(BF16)
                onward_copy(k).start()

        for q in range(rows):
            esend[k, q] = (fades[q] * pin[k].astype(F32) + before[q]).astype(BF16)
        for d in range(1, rows):
            enter_copy(k, d).start()
        enter[k, r] = esend[k, r]
        return carry

    ticks = users * stretches

    def due(t):
        reach = (2 * t + 1 - 4 * c + 3 * 4 * cols) // 3 - 4 * cols + 1
        return jnp.minimum(jnp.maximum(reach, 0), pieces)

    wgate_copy.wait()
    chunk = inner // stretches

    def local_step(t, done):
        now = due(t)
        lax.fori_loop(done, now, handle, 0)
        u, s = t // stretches, lax.rem(t, stretches)
        span = pl.ds(pl.multiple_of(s * chunk, chunk), chunk)
        mine = pl.ds(pl.multiple_of(u * events, events), events)

        @pl.when(u == 0)
        def _():
            tgate[:, span] = jnp.dot(
                table[...], wgate[:, span], preferred_element_type=F32
            ).astype(BF16)

        gates[mine, span] = silu(
            jnp.dot(hot[u, pl.ds(HALO, events), :], tgate[:, span], preferred_element_type=F32)
        )
        base = pl.multiple_of(s * STRETCH, STRETCH)
        place_rows = pl.ds(pl.multiple_of(u * events + s * STRETCH, STRETCH), STRETCH)
        seen = outward[place_rows, :]
        scores = jnp.dot(
            seen, inward_t[u, :, pl.ds(base, STRETCH)], preferred_element_type=F32
        )
        scores = jnp.where(causal, scores, 0.0)
        log = logs[u, pl.ds(base, STRETCH), :]
        fade = jnp.exp(-log)
        wide_seen = seen.astype(F32)
        for p in range(heads):
            h = head_of(p)
            gap = jnp.minimum(logs_t[u, s, p : p + 1, :] - log[:, p : p + 1], 0.0)
            weights = (jnp.exp(gap) * (scores * steps_t[u, s, p : p + 1, :])).astype(BF16)
            faded = (wide_seen * fade[:, p : p + 1]).astype(BF16)
            q = p % rows
            right = jnp.concatenate(
                [
                    signal[u, p, pl.ds(base, STRETCH), :],
                    held[u * per + p // rows, s, :, q * LANES : (q + 1) * LANES],
                ],
                axis=0,
            )
            y[place_rows, h * LANES : (h + 1) * LANES] = jnp.dot(
                jnp.concatenate([weights, faded], axis=1), right, preferred_element_type=F32
            )
        return now

    done = lax.fori_loop(0, ticks, local_step, 0)
    lax.fori_loop(done, pieces, handle, 0)
    wout_copy.wait()
    tiles = events // tall

    def out_copy(i):
        span = pl.ds(pl.multiple_of(i * tall, tall), tall)
        return pltpu.make_async_copy(ostage.at[span, :], out_ref.at[span, :], osem.at[i])

    def finish_step(i, carry):
        u = i // tiles

        @pl.when(lax.rem(i, tiles) == 0)
        def _():
            for j in range(per):
                for d in range(1, rows):
                    enter_copy(u * per + j, d).wait_recv()

        span = pl.ds(pl.multiple_of(i * tall, tall), tall)
        squares = None
        for p in range(0, heads, 2):
            far = jnp.dot(
                outward[span, :],
                jnp.concatenate(
                    [enter[u * per + e // rows, e % rows] for e in (p, p + 1)], axis=1
                ),
                preferred_element_type=F32,
            )
            for e in (p, p + 1):
                h = head_of(e)
                where = slice(h * LANES, (h + 1) * LANES)
                part = far[:, (e - p) * LANES : (e - p + 1) * LANES]
                value = (y[span, where] + part * ef[span, e : e + 1]) * gates[span, where]
                mix[:, where] = value
                squares = value * value if squares is None else squares + value * value
        mean = jnp.sum(squares, axis=1, keepdims=True) * (1.0 / inner)
        normed = (mix[...] * lax.rsqrt(mean + 1.0) * gain_ref[...]).astype(BF16)
        result = jnp.dot(normed, wout[...], preferred_element_type=F32)
        ostage[span, :] = (result * ef[span, LANES - 1 : LANES]).astype(BF16)
        out_copy(i).start()
        return carry

    lax.fori_loop(0, users * tiles, finish_step, 0)

    @pl.when(has_after)
    def _():
        halo_copy.wait_send()

    for u in range(users):
        for d in range(1, rows):
            log_copy(u, d).wait_send()
    for k in range(pieces):
        for d in range(1, rows):
            state_copy(k, d).wait_send()
            enter_copy(k, d).wait_send()
    if cols > 1:

        @pl.when(c < cols - 1)
        def _():
            for k in range(pieces):
                onward_copy(k).wait_send()

    for i in range(users * tiles):
        out_copy(i).wait()


def per_device(
    item_ids,
    pad_masks,
    lengths,
    item_table,
    w_gate,
    w_in,
    w_dt,
    conv_taps,
    dt_bias,
    decay_rates,
    norm_gain,
    w_out,
):
    users, _, events = item_ids.shape
    items, model = item_table.shape
    full_width = w_in.shape[1]
    inner = w_gate.shape[1]
    heads = decay_rates.shape[0]
    state_width = (full_width - inner) // 2
    rows, cols = lax.axis_size("row"), lax.axis_size("col")
    stretches = events // STRETCH
    per = heads // rows
    pieces = users * per
    total = users * events
    tall = 2 * STRETCH if events % (2 * STRETCH) == 0 else STRETCH
    group = rows * LANES
    head = (state_width, LANES)

    vmem = pl.BlockSpec(memory_space=pltpu.VMEM)
    hbm = pl.BlockSpec(memory_space=pl.ANY)
    dma = pltpu.SemaphoreType.DMA

    def f32(*shape):
        return pltpu.VMEM(shape, F32)

    def bf16(*shape):
        return pltpu.VMEM(shape, BF16)

    result = pl.pallas_call(
        functools.partial(mixer_kernel, (rows, cols, users, heads, tall)),
        in_specs=[pl.BlockSpec(memory_space=pltpu.SMEM)] + [vmem] * 7 + [hbm] * 4,
        out_specs=hbm,
        out_shape=jax.ShapeDtypeStruct((total, w_out.shape[1]), BF16),
        scratch_shapes=[
            bf16(items, model),
            bf16(model, full_width),
            bf16(model, inner),
            bf16(*w_out.shape),
            bf16(items, full_width),
            bf16(items, inner),
            bf16(items, LANES),
            bf16(LANES, model),
            f32(8, LANES),
            f32(heads + 2, 8, LANES),
            bf16(users, HALO + events, items),
            f32(max(rows, 2), HALO + events, LANES),
            bf16(users, state_width, events),
            bf16(total, state_width),
            f32(users, events, LANES),
            f32(users, stretches, 8, LANES),
            f32(users, stretches, 8, LANES),
            f32(pieces, events, LANES),
            f32(pieces, stretches, 8, group),
            f32(total, LANES),
            bf16(users, heads, events, LANES),
            bf16(events, group),
            bf16(pieces, stretches, state_width, group),
            bf16(pieces, rows, *head),
            bf16(pieces, rows, *head),
            f32(users, rows, per, 8, LANES),
            f32(users, rows, per, 8, LANES),
            f32(rows, *head),
            bf16(pieces, *head),
            bf16(pieces, *head),
            bf16(pieces, rows, *head),
            bf16(pieces, rows, *head),
            f32(total, inner),
            f32(total, inner),
            f32(tall, inner),
            bf16(total, w_out.shape[1]),
            pltpu.VMEM((users, 1, STRETCH), jnp.int32),
            dma((heads + 5,)),
            dma((total // tall,)),
            dma((2,)),
            dma((1,)),
            dma((users, rows)),
            dma((users, rows)),
            dma((pieces, rows)),
            dma((pieces, rows)),
            dma((pieces,)),
            dma((pieces,)),
            dma((pieces, rows)),
            dma((pieces, rows)),
        ],
        compiler_params=pltpu.CompilerParams(
            collective_id=0, has_side_effects=True, vmem_limit_bytes=56 * 1024 * 1024
        ),
        name="mixer",
    )(
        lengths,
        item_ids,
        pad_masks,
        w_dt.T,
        conv_taps,
        dt_bias[None],
        decay_rates[None],
        norm_gain[None],
        item_table,
        w_in,
        w_gate,
        w_out,
    )
    return result.reshape(users, 1, events, -1)


def solution(mesh):
    in_specs = (
        P("batch", "col", "row"),
        P("batch", "col", "row"),
        P("batch"),
        P(),
        P(),
        P(),
        P(),
        P(),
        P(),
        P(),
        P(),
        P(),
    )
    out_specs = P("batch", "col", "row", None)
    return jax.shard_map(
        per_device, mesh=mesh, in_specs=in_specs, out_specs=out_specs, check_vma=False
    )
```

time: 61.4 us -> 39.1 us (0.64)
  Pallas kernels: 61.1 us -> 35.7 us
  local copies, waits for them, and re-layouts: 0 us -> 3.08 us
    pallas_call x4 -> x1, Pallas kernels: 61.1 us -> 35.7 us  [per_device(): pl.pallas_call(functools.partial(mixer_kernel, (rows, cols, users, heads,...]
    unnamed x0 -> x1, local copies, waits for them, and re-layouts: none -> 3.08 us
where the time goes in v1:
time: 39.1 us; the launch traced here: 38.8 us
  Pallas kernels  35.7 us (91%)
  local copies, waits for them, and re-layouts  3.08 us (8%)
    pallas_call x1, Pallas kernels, per_device(): pl.pallas_call(functools.partial(mixer_kernel, (rows, cols, users, heads,...  35.7 us
    unnamed x1, local copies, waits for them, and re-layouts  3.08 us

profile of v1, /device:TPU:24, one launch (start us, length us, event | category | flops | bytes accessed | tf_op | source)
XLA Modules:
  0.0 38.8 jit_solution(13585337461609839820)
XLA Ops:
  0.0 35.7 %mixer.1 = bf16[1024,1024]{1,0:T(8,128)(2,1)} custom-call(s32[2]{0:T(128)} %lengths_ref.1, s32[2,1,512]{2,1,0:T(1,128)} %ids_ref.1, s32[2,1,512]{2,1,0:T(1,128)} %masks_ref.1, bf16[8,1024]{1,0:T(8,128)(2,1)} %bitcast.8, f32[4,1280]{1,0:T(4,128)} %taps_ref.1, f32[1,8]{1,0:T(1,128)} %bitcast.10, f32[1,8]{1,0:T(1,128)} %bitcast.11, f32[1,1024]{1,0:T(1,128)} %bitcast.9, ...), custom_call_target="tpu_custom_call" | custom-call | tf_op jit(solution)/shard_map/mixer/pallas_call | solution.py:563
  35.7 3.1 %copy.15 = bf16[2,1,512,1024]{3,2,1,0:T(8,128)(2,1)} copy(bf16[2,1,512,1024]{3,2,1,0:T(8,128)(2,1)} %bitcast.7) | data formatting | bytes 4194304

commit v2 on v1

--- a/solution.py
+++ b/solution.py
@@ -32,6 +32,19 @@
 
 def mixer_kernel(
     counts,
+    lengths_hbm,
+    ids_hbm,
+    masks_hbm,
+    wdt_hbm,
+    taps_hbm,
+    bias_hbm,
+    rates_hbm,
+    gain_hbm,
+    table_hbm,
+    win_hbm,
+    wgate_hbm,
+    wout_hbm,
+    out_ref,
     lengths_ref,
     ids_ref,
     masks_ref,
@@ -40,11 +53,6 @@
     bias_ref,
     rates_ref,
     gain_ref,
-    table_hbm,
-    win_hbm,
-    wgate_hbm,
-    wout_hbm,
-    out_ref,
     table,
     win,
     wgate,
@@ -59,12 +67,10 @@
     rowbuf,
     inward_t,
     outward,
-    logs,
+    facts,
     logs_t,
     steps_t,
-    tails,
     shrinks,
-    ef,
     signal,
     scaled,
     held,
@@ -80,12 +86,10 @@
     y,
     gates,
     mix,
-    ostage,
     landed,
     wsem,
-    osem,
+    psem,
     hsem,
-    ssem,
     lsem_s,
     lsem_r,
     s1,
@@ -129,7 +133,24 @@
     table_copy = pltpu.make_async_copy(table_hbm, table, wsem.at[blocks])
     wgate_copy = pltpu.make_async_copy(wgate_hbm, wgate, wsem.at[blocks + 1])
     wout_copy = pltpu.make_async_copy(wout_hbm, wout, wsem.at[blocks + 2])
+    small = [
+        pltpu.make_async_copy(source, target, psem.at[i])
+        for i, (source, target) in enumerate(
+            (
+                (ids_hbm, ids_ref),
+                (masks_hbm, masks_ref),
+                (lengths_hbm, lengths_ref),
+                (wdt_hbm, wdt_ref),
+                (taps_hbm, taps_ref),
+                (bias_hbm, bias_ref),
+                (rates_hbm, rates_ref),
+                (gain_hbm, gain_ref),
+            )
+        )
+    ]
     table_copy.start()
+    for copy in small:
+        copy.start()
     for p in (heads, heads + 1, *range(heads)):
         column(p).start()
     wgate_copy.start()
@@ -161,12 +182,17 @@
         ids_ref.at[:, :, pl.ds(events - STRETCH, STRETCH)], landed, hsem.at[0], hsem.at[1], after
     )
 
-    params[...] = jnp.zeros_like(params)
     wide[...] = jnp.zeros_like(wide)
-    for p in range(heads):
-        h = head_of(p)
-        params[0:1, p : p + 1] = bias_ref[:, h : h + 1]
-        params[1:2, p : p + 1] = rates_ref[:, h : h + 1]
+    for copy in small:
+        copy.wait()
+    line_rows = lax.broadcasted_iota(jnp.int32, (STRETCH, STRETCH), 0)
+    line_cols = lax.broadcasted_iota(jnp.int32, (STRETCH, STRETCH), 1)
+    causal = line_rows >= line_cols
+    for i, source in enumerate((bias_ref, rates_ref)):
+        value = jnp.zeros((heads, LANES), F32)
+        for p in range(heads):
+            value = jnp.where(line_rows[0:heads] == p, source[:, head_of(p) : head_of(p) + 1], value)
+        params[i] = value
     wide[0:heads, :] = jnp.concatenate(
         [wdt_ref[head_of(p) : head_of(p) + 1, :] for p in range(heads)], axis=0
     )
@@ -185,6 +211,14 @@
     column(heads).wait()
     column(heads + 1).wait()
     table_block(heads * LANES)
+
+    raw = lax.dot_general(
+        table[...], wide[...], (((1,), (1,)), ((), ())), preferred_element_type=F32
+    )
+    high = raw.astype(BF16).astype(F32)
+    middle = (raw - high).astype(BF16).astype(F32)
+    low = raw - high - middle
+    tdt[...] = (high + pltpu.roll(middle, heads, 1) + pltpu.roll(low, 2 * heads, 1)).astype(BF16)
 
     peers = (
         rows
@@ -200,14 +234,6 @@
     def _():
         halo_copy.start()
 
-    raw = lax.dot_general(
-        table[...], wide[...], (((1,), (1,)), ((), ())), preferred_element_type=F32
-    )
-    high = raw.astype(BF16).astype(F32)
-    middle = (raw - high).astype(BF16).astype(F32)
-    low = raw - high - middle
-    tdt[...] = (high + pltpu.roll(middle, heads, 1) + pltpu.roll(low, 2 * heads, 1)).astype(BF16)
-
     for p in range(heads):
         column(p).wait()
 
@@ -216,6 +242,16 @@
         return carry
 
     lax.fori_loop(0, heads // 2, table_step, 0)
+    wgate_copy.wait()
+
+    def gate_step(i, carry):
+        span = pl.ds(pl.multiple_of(i * 2 * LANES, 2 * LANES), 2 * LANES)
+        tgate[:, span] = jnp.dot(
+            table[...], wgate[:, span], preferred_element_type=F32
+        ).astype(BF16)
+        return carry
+
+    lax.fori_loop(0, inner // (2 * LANES), gate_step, 0)
 
     @pl.when(place == 0)
     def _():
@@ -224,10 +260,6 @@
     @pl.when(has_before)
     def _():
         halo_copy.wait_recv()
-
-    line_rows = lax.broadcasted_iota(jnp.int32, (STRETCH, STRETCH), 0)
-    line_cols = lax.broadcasted_iota(jnp.int32, (STRETCH, STRETCH), 1)
-    causal = line_rows >= line_cols
 
     def convolve(position, slot):
         total = None
@@ -264,7 +296,6 @@
         flags = jnp.concatenate([jnp.zeros((1, STRETCH), F32), kept], axis=1)
         line = lax.broadcasted_iota(jnp.int32, (8, STRETCH + events), 0)
         meta = jnp.transpose(jnp.where(line == 0, names, jnp.where(line == 1, flags, 0.0)))
-        usable = meta[STRETCH:, 1:2]
         ids = meta[STRETCH - HALO :, 0:1].astype(jnp.int32)
         items = table.shape[0]
         lane = lax.broadcasted_iota(jnp.int32, (HALO + events, items), 1)
@@ -273,61 +304,68 @@
         rowbuf[0] = both[:, :LANES]
         rowbuf[1] = both[:, LANES:]
         parts = jnp.dot(hot[u, pl.ds(HALO, events), :], tdt[...], preferred_element_type=F32)
-        raw = (
-            parts
-            + pltpu.roll(parts, LANES - heads, 1)
-            + pltpu.roll(parts, LANES - 2 * heads, 1)
-        )
-        raw = raw + params[0:1, :]
-        step = usable * (jnp.maximum(raw, 0.0) + jnp.log1p(jnp.exp(-jnp.abs(raw))))
-        paced = step * params[1:2, :]
+        parts = jnp.transpose(parts)
+        raw = parts[0:heads] + parts[heads : 2 * heads] + parts[2 * heads : 3 * heads]
+        upper = jnp.where(line_rows <= line_cols, 1.0, 0.0).astype(F32)
+        steps, paced = [], []
+        for s in range(stretches):
+            span = slice(s * STRETCH, (s + 1) * STRETCH)
+            value = raw[:, span] + params[0]
+            step = kept[:, span] * (jnp.maximum(value, 0.0) + jnp.log1p(jnp.exp(-jnp.abs(value))))
+            steps.append(step)
+            paced.append(step * params[1])
+        sums = jnp.dot(
+            jnp.concatenate(paced, axis=0),
+            upper,
+            precision=lax.Precision.HIGHEST,
+            preferred_element_type=F32,
+        )
+        past = jnp.zeros((heads, LANES), F32)
+        for s in range(stretches):
+            log = sums[s * heads : (s + 1) * heads]
+            step = steps[s]
+            logs_t[u, s] = log
+            steps_t[u, s] = step
+            total = jnp.broadcast_to(log[:, STRETCH - 1 :], (heads, LANES))
+            tail = jnp.exp(log - total) * step
+            shrink = jnp.exp(-total)
+            for p in range(heads):
+                shrinks[u * per + p // rows, s, :, (p % rows) * LANES : (p % rows + 1) * LANES] = (
+                    jnp.broadcast_to(shrink[p : p + 1], (8, LANES))
+                )
+            used = jnp.broadcast_to(kept[:, s * STRETCH : (s + 1) * STRETCH], (heads, LANES))
+            facts[pl.ds(pl.multiple_of(u * events + s * STRETCH, STRETCH), STRETCH), :] = jnp.transpose(
+                jnp.concatenate(
+                    [log, tail, jnp.exp(-log), jnp.exp(-(log + past)), used]
+                    + [jnp.zeros((LANES - 5 * heads, LANES), F32)],
+                    axis=0,
+                )
+            )
+            past = past + total
+        for p in range(heads):
+            aft[u, p % rows, p // rows] = jnp.broadcast_to(past[p : p + 1], (8, LANES))
         inward_t[u] = jnp.transpose(convolve(heads, 0)).astype(BF16)
         outward[pl.ds(pl.multiple_of(u * events, events), events), :] = convolve(heads + 1, 1).astype(BF16)
-        past = jnp.zeros((1, LANES), F32)
-        lower = jnp.where(causal, 1.0, 0.0).astype(F32)
-        for s in range(stretches):
-            span = slice(s * STRETCH, (s + 1) * STRETCH)
-            log = jnp.dot(
-                lower, paced[span], precision=lax.Precision.HIGHEST, preferred_element_type=F32
-            )
-            logs[u, span, :] = log
-            logs_t[u, s] = jnp.transpose(log)[0:8, :]
-            steps_t[u, s] = jnp.transpose(step[span])[0:8, :]
-            total = log[STRETCH - 1 :, :]
-            tail = jnp.exp(log - total) * step[span]
-            shrink = jnp.exp(-total)
-            for j in range(per):
-                turned = tail if j == 0 else pltpu.roll(tail, LANES - j * rows, 1)
-                tails[u * per + j, span, :] = turned
-                for q in range(rows):
-                    p = j * rows + q
-                    shrinks[u * per + j, s, :, q * LANES : (q + 1) * LANES] = jnp.broadcast_to(
-                        shrink[:, p : p + 1], (8, LANES)
-                    )
-            lane = lax.broadcasted_iota(jnp.int32, (STRETCH, LANES), 1)
-            ef[pl.ds(pl.multiple_of(u * events + s * STRETCH, STRETCH), STRETCH), :] = jnp.where(
-                lane == LANES - 1, usable[span], jnp.exp(-(log + past))
-            )
-            past = past + total
-        for q in range(rows):
-            for j in range(per):
-                p = j * rows + q
-                aft[u, q, j] = jnp.broadcast_to(past[:, p : p + 1], (8, LANES))
         for d in range(1, rows):
             log_copy(u, d).start()
         lin[u, r] = aft[u, r]
 
     def group(u, j):
         k = u * per + j
-        base = pl.multiple_of(j * wide_group, wide_group)
-        gathered = jnp.dot(hot[u], tin[:, pl.ds(base, wide_group)], preferred_element_type=F32)
+        mine = pl.ds(pl.multiple_of(u * events, events), events)
+        gathered = jnp.dot(
+            hot[u], tin[:, j * wide_group : (j + 1) * wide_group], preferred_element_type=F32
+        )
         for q in range(rows):
             rowbuf[q] = gathered[:, q * LANES : (q + 1) * LANES]
         for q in range(rows):
             span = slice(q * LANES, (q + 1) * LANES)
             value = silu(convolve(j * rows + q, q)).astype(BF16)
             signal[u, j * rows + q] = value
-            scaled[:, span] = (value.astype(F32) * tails[k, :, q : q + 1]).astype(BF16)
+            scaled[:, span] = (
+                value.astype(F32)
+                * facts[mine, heads + j * rows + q : heads + j * rows + q + 1]
+            ).astype(BF16)
         run = None
         for s in range(stretches):
             span = slice(s * STRETCH, (s + 1) * STRETCH)
@@ -347,12 +385,9 @@
 
     def user_step(u, carry):
         prepare(u)
-
-        def group_step(j, inner_carry):
+        for j in range(per):
             group(u, j)
-            return inner_carry
-
-        return lax.fori_loop(0, per, group_step, carry)
+        return carry
 
     lax.fori_loop(0, users, user_step, 0)
 
@@ -408,7 +443,6 @@
         reach = (2 * t + 1 - 4 * c + 3 * 4 * cols) // 3 - 4 * cols + 1
         return jnp.minimum(jnp.maximum(reach, 0), pieces)
 
-    wgate_copy.wait()
     chunk = inner // stretches
 
     def local_step(t, done):
@@ -418,12 +452,6 @@
         span = pl.ds(pl.multiple_of(s * chunk, chunk), chunk)
         mine = pl.ds(pl.multiple_of(u * events, events), events)
 
-        @pl.when(u == 0)
-        def _():
-            tgate[:, span] = jnp.dot(
-                table[...], wgate[:, span], preferred_element_type=F32
-            ).astype(BF16)
-
         gates[mine, span] = silu(
             jnp.dot(hot[u, pl.ds(HALO, events), :], tgate[:, span], preferred_element_type=F32)
         )
@@ -434,14 +462,13 @@
             seen, inward_t[u, :, pl.ds(base, STRETCH)], preferred_element_type=F32
         )
         scores = jnp.where(causal, scores, 0.0)
-        log = logs[u, pl.ds(base, STRETCH), :]
-        fade = jnp.exp(-log)
+        known = facts[place_rows, :]
         wide_seen = seen.astype(F32)
         for p in range(heads):
             h = head_of(p)
-            gap = jnp.minimum(logs_t[u, s, p : p + 1, :] - log[:, p : p + 1], 0.0)
+            gap = jnp.minimum(logs_t[u, s, p : p + 1, :] - known[:, p : p + 1], 0.0)
             weights = (jnp.exp(gap) * (scores * steps_t[u, s, p : p + 1, :])).astype(BF16)
-            faded = (wide_seen * fade[:, p : p + 1]).astype(BF16)
+            faded = (wide_seen * known[:, 2 * heads + p : 2 * heads + p + 1]).astype(BF16)
             q = p % rows
             right = jnp.concatenate(
                 [
@@ -458,46 +485,37 @@
     done = lax.fori_loop(0, ticks, local_step, 0)
     lax.fori_loop(done, pieces, handle, 0)
     wout_copy.wait()
-    tiles = events // tall
-
-    def out_copy(i):
-        span = pl.ds(pl.multiple_of(i * tall, tall), tall)
-        return pltpu.make_async_copy(ostage.at[span, :], out_ref.at[span, :], osem.at[i])
-
-    def finish_step(i, carry):
-        u = i // tiles
-
-        @pl.when(lax.rem(i, tiles) == 0)
-        def _():
-            for j in range(per):
-                for d in range(1, rows):
-                    enter_copy(u * per + j, d).wait_recv()
-
-        span = pl.ds(pl.multiple_of(i * tall, tall), tall)
-        squares = None
-        for p in range(0, heads, 2):
-            far = jnp.dot(
-                outward[span, :],
-                jnp.concatenate(
-                    [enter[u * per + e // rows, e % rows] for e in (p, p + 1)], axis=1
-                ),
-                preferred_element_type=F32,
-            )
-            for e in (p, p + 1):
-                h = head_of(e)
-                where = slice(h * LANES, (h + 1) * LANES)
-                part = far[:, (e - p) * LANES : (e - p + 1) * LANES]
-                value = (y[span, where] + part * ef[span, e : e + 1]) * gates[span, where]
-                mix[:, where] = value
-                squares = value * value if squares is None else squares + value * value
-        mean = jnp.sum(squares, axis=1, keepdims=True) * (1.0 / inner)
-        normed = (mix[...] * lax.rsqrt(mean + 1.0) * gain_ref[...]).astype(BF16)
-        result = jnp.dot(normed, wout[...], preferred_element_type=F32)
-        ostage[span, :] = (result * ef[span, LANES - 1 : LANES]).astype(BF16)
-        out_copy(i).start()
+
+    def finish_step(u, carry):
+        for j in range(per):
+            for d in range(1, rows):
+                enter_copy(u * per + j, d).wait_recv()
+        for i in range(events // tall):
+            span = pl.ds(pl.multiple_of(u * events + i * tall, tall), tall)
+            squares = None
+            for p in range(0, heads, 2):
+                far = jnp.dot(
+                    outward[span, :],
+                    jnp.concatenate(
+                        [enter[u * per + e // rows, e % rows] for e in (p, p + 1)], axis=1
+                    ),
+                    preferred_element_type=F32,
+                )
+                for e in (p, p + 1):
+                    h = head_of(e)
+                    where = slice(h * LANES, (h + 1) * LANES)
+                    part = far[:, (e - p) * LANES : (e - p + 1) * LANES]
+                    fade = facts[span, 3 * heads + e : 3 * heads + e + 1]
+                    value = (y[span, where] + part * fade) * gates[span, where]
+                    mix[i, :, where] = value
+                    squares = value * value if squares is None else squares + value * value
+            mean = jnp.sum(squares, axis=1, keepdims=True) * (1.0 / inner)
+            normed = (mix[i] * lax.rsqrt(mean + 1.0) * gain_ref[...]).astype(BF16)
+            result = jnp.dot(normed, wout[...], preferred_element_type=F32)
+            out_ref[span, :] = (result * facts[span, 4 * heads : 4 * heads + 1]).astype(BF16)
         return carry
 
-    lax.fori_loop(0, users * tiles, finish_step, 0)
+    lax.fori_loop(0, users, finish_step, 0)
 
     @pl.when(has_after)
     def _():
@@ -516,9 +534,6 @@
         def _():
             for k in range(pieces):
                 onward_copy(k).wait_send()
-
-    for i in range(users * tiles):
-        out_copy(i).wait()
 
 
 def per_device(
@@ -551,7 +566,7 @@
     head = (state_width, LANES)
 
     vmem = pl.BlockSpec(memory_space=pltpu.VMEM)
-    hbm = pl.BlockSpec(memory_space=pl.ANY)
+    hbm = pl.BlockSpec(memory_space=pltpu.HBM)
     dma = pltpu.SemaphoreType.DMA
 
     def f32(*shape):
@@ -562,10 +577,18 @@
 
     result = pl.pallas_call(
         functools.partial(mixer_kernel, (rows, cols, users, heads, tall)),
-        in_specs=[pl.BlockSpec(memory_space=pltpu.SMEM)] + [vmem] * 7 + [hbm] * 4,
-        out_specs=hbm,
+        in_specs=[hbm] * 12,
+        out_specs=vmem,
         out_shape=jax.ShapeDtypeStruct((total, w_out.shape[1]), BF16),
         scratch_shapes=[
+            pltpu.SMEM(lengths.shape, jnp.int32),
+            pltpu.VMEM(item_ids.shape, jnp.int32),
+            pltpu.VMEM(pad_masks.shape, jnp.int32),
+            bf16(*w_dt.shape[::-1]),
+            f32(*conv_taps.shape),
+            f32(1, heads),
+            f32(1, heads),
+            f32(1, inner),
             bf16(items, model),
             bf16(model, full_width),
             bf16(model, inner),
@@ -574,18 +597,16 @@
             bf16(items, inner),
             bf16(items, LANES),
             bf16(LANES, model),
-            f32(8, LANES),
+            f32(2, heads, LANES),
             f32(heads + 2, 8, LANES),
             bf16(users, HALO + events, items),
             f32(max(rows, 2), HALO + events, LANES),
             bf16(users, state_width, events),
             bf16(total, state_width),
-            f32(users, events, LANES),
-            f32(users, stretches, 8, LANES),
-            f32(users, stretches, 8, LANES),
-            f32(pieces, events, LANES),
+            f32(total, LANES),
+            f32(users, stretches, heads, LANES),
+            f32(users, stretches, heads, LANES),
             f32(pieces, stretches, 8, group),
-            f32(total, LANES),
             bf16(users, heads, events, LANES),
             bf16(events, group),
             bf16(pieces, stretches, state_width, group),
@@ -600,13 +621,11 @@
             bf16(pieces, rows, *head),
             f32(total, inner),
             f32(total, inner),
-            f32(tall, inner),
-            bf16(total, w_out.shape[1]),
+            f32(events // tall, tall, inner),
             pltpu.VMEM((users, 1, STRETCH), jnp.int32),
             dma((heads + 5,)),
-            dma((total // tall,)),
+            dma((8,)),
             dma((2,)),
-            dma((1,)),
             dma((users, rows)),
             dma((users, rows)),
             dma((pieces, rows)),
@@ -617,22 +636,27 @@
             dma((pieces, rows)),
         ],
         compiler_params=pltpu.CompilerParams(
-            collective_id=0, has_side_effects=True, vmem_limit_bytes=56 * 1024 * 1024
+            collective_id=0, has_side_effects=True, vmem_limit_bytes=48 * 1024 * 1024
         ),
         name="mixer",
     )(
-        lengths,
-        item_ids,
-        pad_masks,
-        w_dt.T,
-        conv_taps,
-        dt_bias[None],
-        decay_rates[None],
-        norm_gain[None],
-        item_table,
-        w_in,
-        w_gate,
-        w_out,
+        *(
+            pltpu.with_memory_space_constraint(array, pltpu.HBM)
+            for array in (
+                lengths,
+                item_ids,
+                pad_masks,
+                w_dt.T,
+                conv_taps,
+                dt_bias[None],
+                decay_rates[None],
+                norm_gain[None],
+                item_table,
+                w_in,
+                w_gate,
+                w_out,
+            )
+        )
     )
     return result.reshape(users, 1, events, -1)
 

time: 39.1 us -> 35.6 us (0.910)
  local copies, waits for them, and re-layouts: 3.08 us -> 1.32 us
  Pallas kernels: 35.7 us -> 34.2 us
    unnamed x1, local copies, waits for them, and re-layouts: 3.08 us -> 1.32 us
    pallas_call x1, Pallas kernels: 35.7 us -> 34.2 us  [per_device(): pl.pallas_call(functools.partial(mixer_kernel, (rows, cols, users, heads,...]
where the time goes in v2:
time: 35.6 us; the launch traced here: 35.5 us
  Pallas kernels  34.2 us (96%)
  local copies, waits for them, and re-layouts  1.32 us (4%)
    pallas_call x1, Pallas kernels, per_device(): pl.pallas_call(functools.partial(mixer_kernel, (rows, cols, users, heads,...  34.2 us
    unnamed x1, local copies, waits for them, and re-layouts  1.32 us

profile of v2, /device:TPU:24, one launch (start us, length us, event | category | flops | bytes accessed | tf_op | source)
XLA Modules:
  0.0 35.5 jit_solution(17898313763553889899)
XLA Ops:
  0.0 34.2 %mixer.1 = bf16[1024,1024]{1,0:T(8,128)(2,1)S(1)} custom-call(s32[2]{0:T(128)} %lengths_hbm.1, s32[2,1,512]{2,1,0:T(1,128)} %ids_hbm.1, s32[2,1,512]{2,1,0:T(1,128)} %masks_hbm.1, bf16[8,1024]{1,0:T(8,128)(2,1)} %bitcast.8, f32[4,1280]{1,0:T(4,128)} %taps_hbm.1, f32[1,8]{1,0:T(1,128)} %bitcast.10, f32[1,8]{1,0:T(1,128)} %bitcast.11, f32[1,1024]{1,0:T(1,128)} %bitcast.9, ...), custom_call_target="tpu_custom_call" | custom-call | tf_op jit(solution)/shard_map/mixer/pallas_call | solution.py:578
  34.2 1.3 %copy.15 = bf16[2,1,512,1024]{3,2,1,0:T(8,128)(2,1)} copy(bf16[2,1,512,1024]{3,2,1,0:T(8,128)(2,1)S(1)} %bitcast.7) | data formatting | bytes 4194304

commit v3 on v2

--- a/solution.py
+++ b/solution.py
@@ -79,13 +79,19 @@
     aft,
     lin,
     before,
+    fades,
     pin,
+    nearin,
+    farin,
+    fadein,
     psend,
+    fsend,
     esend,
     enter,
     y,
     gates,
     mix,
+    sums,
     landed,
     wsem,
     psem,
@@ -98,6 +104,10 @@
     r2,
     s3,
     r3,
+    s4,
+    r4,
+    s5,
+    r5,
 ):
     rows, cols, users, heads, tall = counts
     events = ids_ref.shape[2]
@@ -122,7 +132,7 @@
         return (p % rows) * per + p // rows
 
     def column(p):
-        source = p if p >= heads else head_of(p)
+        source = head_of(p) if not isinstance(p, int) or p < heads else p
         return pltpu.make_async_copy(
             win_hbm.at[:, pl.ds(source * LANES, LANES)],
             win.at[:, pl.ds(p * LANES, LANES)],
@@ -153,8 +163,6 @@
         copy.start()
     for p in (heads, heads + 1, *range(heads)):
         column(p).start()
-    wgate_copy.start()
-    wout_copy.start()
 
     barrier = pltpu.get_barrier_semaphore()
     for d in range(1, rows):
@@ -169,6 +177,14 @@
     @pl.when(c < cols - 1)
     def _():
         pl.semaphore_signal(barrier, inc=1, device_id={"col": c + 1}, device_id_type=MESH)
+
+    @pl.when(c > 1)
+    def _():
+        pl.semaphore_signal(barrier, inc=1, device_id={"col": c - 2}, device_id_type=MESH)
+
+    @pl.when(c < cols - 2)
+    def _():
+        pl.semaphore_signal(barrier, inc=1, device_id={"col": c + 2}, device_id_type=MESH)
 
     @pl.when(wraps)
     def _():
@@ -225,6 +241,8 @@
         - 1
         + jnp.where(c > 0, 1, 0)
         + jnp.where(c < cols - 1, 1, 0)
+        + jnp.where(c > 1, 1, 0)
+        + jnp.where(c < cols - 2, 1, 0)
         + jnp.where(wraps, 1, 0)
         + jnp.where(wrapped, 1, 0)
     )
@@ -234,24 +252,15 @@
     def _():
         halo_copy.start()
 
-    for p in range(heads):
-        column(p).wait()
-
     def table_step(i, carry):
+        column(2 * i).wait()
+        column(2 * i + 1).wait()
         table_block(i * 2 * LANES)
         return carry
 
     lax.fori_loop(0, heads // 2, table_step, 0)
-    wgate_copy.wait()
-
-    def gate_step(i, carry):
-        span = pl.ds(pl.multiple_of(i * 2 * LANES, 2 * LANES), 2 * LANES)
-        tgate[:, span] = jnp.dot(
-            table[...], wgate[:, span], preferred_element_type=F32
-        ).astype(BF16)
-        return carry
-
-    lax.fori_loop(0, inner // (2 * LANES), gate_step, 0)
+    wgate_copy.start()
+    wout_copy.start()
 
     @pl.when(place == 0)
     def _():
@@ -278,9 +287,19 @@
         q = lax.rem(r + d, rows)
         return remote(ssend.at[k, q], rin.at[k, r], s1.at[k, d], r1.at[k, d], {"row": q})
 
-    def onward_copy(k):
+    def near_copy(k):
         return remote(
-            psend.at[k], pin.at[k], s2.at[k], r2.at[k], {"col": lax.rem(c + 1, cols)}
+            psend.at[k], nearin.at[k], s2.at[k], r2.at[k], {"col": lax.rem(c + 1, cols)}
+        )
+
+    def fade_copy(k):
+        return remote(
+            fsend.at[k], fadein.at[k], s4.at[k], r4.at[k], {"col": lax.rem(c + 1, cols)}
+        )
+
+    def far_copy(k):
+        return remote(
+            psend.at[k], farin.at[k], s5.at[k], r5.at[k], {"col": lax.rem(c + 2, cols)}
         )
 
     def enter_copy(k, d):
@@ -391,7 +410,13 @@
 
     lax.fori_loop(0, users, user_step, 0)
 
-    def handle(k, carry):
+    odd = lax.rem(c, 2) == 1
+    gives_own = jnp.logical_and(jnp.logical_not(odd), c < cols - 1)
+    gives_near = jnp.logical_and(odd, c < cols - 1)
+    gives_far = jnp.logical_and(odd, c < cols - 2)
+    takes_far = jnp.logical_and(odd, c > 1)
+
+    def gather_piece(k, carry):
         u, j = k // per, lax.rem(k, per)
         rin[k, r] = ssend[k, r]
 
@@ -402,36 +427,59 @@
 
         for d in range(1, rows):
             state_copy(k, d).wait_recv()
-        carried = jnp.zeros(pin.shape[1:], F32)
-        fade = jnp.ones((1, LANES), F32)
-        fades = []
+        carried = jnp.zeros(nearin.shape[1:], F32)
+        fade = jnp.ones((8, LANES), F32)
         for m in range(rows):
-            before[m] = carried
-            fades.append(fade)
-            here = jnp.exp(-lin[u, m, j, 0:1, :])
-            carried = here * carried + rin[k, m].astype(F32)
+            before[k, m] = carried
+            fades[k, m] = fade
+            here = jnp.exp(-lin[u, m, j])
+            carried = here[0:1] * carried + rin[k, m].astype(F32)
             fade = fade * here
-
+        before[k, rows] = carried
+        fades[k, rows] = fade
+        if cols > 1:
+
+            @pl.when(gives_own)
+            def _():
+                psend[k] = carried.astype(BF16)
+                fsend[k] = fade
+                near_copy(k).start()
+                fade_copy(k).start()
+
+        return carry
+
+    def enter_piece(k, carry):
         @pl.when(c == 0)
         def _():
-            pin[k] = jnp.zeros(pin.shape[1:], BF16)
-            psend[k] = carried.astype(BF16)
-            if cols > 1:
-                onward_copy(k).start()
+            pin[...] = jnp.zeros_like(pin)
 
         if cols > 1:
 
             @pl.when(c > 0)
             def _():
-                onward_copy(k).wait_recv()
-
-            @pl.when(jnp.logical_and(c > 0, c < cols - 1))
+                near_copy(k).wait_recv()
+                pin[...] = nearin[k].astype(F32)
+
+            @pl.when(odd)
             def _():
-                psend[k] = (fade * pin[k].astype(F32) + carried).astype(BF16)
-                onward_copy(k).start()
+                fade_copy(k).wait_recv()
+
+            @pl.when(takes_far)
+            def _():
+                far_copy(k).wait_recv()
+                pin[...] = fadein[k, 0:1] * farin[k].astype(F32) + nearin[k].astype(F32)
+
+            @pl.when(gives_near)
+            def _():
+                psend[k] = (fades[k, rows, 0:1] * pin[...] + before[k, rows]).astype(BF16)
+                near_copy(k).start()
+
+            @pl.when(gives_far)
+            def _():
+                far_copy(k).start()
 
         for q in range(rows):
-            esend[k, q] = (fades[q] * pin[k].astype(F32) + before[q]).astype(BF16)
+            esend[k, q] = (fades[k, q, 0:1] * pin[...] + before[k, q]).astype(BF16)
         for d in range(1, rows):
             enter_copy(k, d).start()
         enter[k, r] = esend[k, r]
@@ -440,17 +488,26 @@
     ticks = users * stretches
 
     def due(t):
-        reach = (2 * t + 1 - 4 * c + 3 * 4 * cols) // 3 - 4 * cols + 1
-        return jnp.minimum(jnp.maximum(reach, 0), pieces)
-
+        return jnp.minimum(jnp.maximum(t, 0) // 2, pieces)
+
+    lag = jnp.where(c == 0, 0, 4 * ((c + 2) // 2))
+
+    wgate_copy.wait()
     chunk = inner // stretches
 
     def local_step(t, done):
-        now = due(t)
-        lax.fori_loop(done, now, handle, 0)
+        now = due(t + 1), due(t + 1 - lag)
+        lax.fori_loop(done[0], now[0], gather_piece, 0)
+        lax.fori_loop(done[1], now[1], enter_piece, 0)
         u, s = t // stretches, lax.rem(t, stretches)
         span = pl.ds(pl.multiple_of(s * chunk, chunk), chunk)
         mine = pl.ds(pl.multiple_of(u * events, events), events)
+
+        @pl.when(u == 0)
+        def _():
+            tgate[:, span] = jnp.dot(
+                table[...], wgate[:, span], preferred_element_type=F32
+            ).astype(BF16)
 
         gates[mine, span] = silu(
             jnp.dot(hot[u, pl.ds(HALO, events), :], tgate[:, span], preferred_element_type=F32)
@@ -482,34 +539,44 @@
             )
         return now
 
-    done = lax.fori_loop(0, ticks, local_step, 0)
-    lax.fori_loop(done, pieces, handle, 0)
+    done = lax.fori_loop(0, ticks, local_step, (0, 0))
+    lax.fori_loop(done[0], pieces, gather_piece, 0)
+    lax.fori_loop(done[1], pieces, enter_piece, 0)
     wout_copy.wait()
 
     def finish_step(u, carry):
+        def rows_of(i):
+            return pl.ds(pl.multiple_of(u * events + i * tall, tall), tall)
+
         for j in range(per):
             for d in range(1, rows):
                 enter_copy(u * per + j, d).wait_recv()
+            for i in range(events // tall):
+                span = rows_of(i)
+                squares = None
+                for q in range(0, rows, 2):
+                    pair = range(q, min(q + 2, rows))
+                    far = jnp.dot(
+                        outward[span, :],
+                        jnp.concatenate([enter[u * per + j, e] for e in pair], axis=1),
+                        preferred_element_type=F32,
+                    )
+                    for e in pair:
+                        h = e * per + j
+                        p = j * rows + e
+                        where = slice(h * LANES, (h + 1) * LANES)
+                        part = far[:, (e - q) * LANES : (e - q + 1) * LANES]
+                        fade = facts[span, 3 * heads + p : 3 * heads + p + 1]
+                        value = (y[span, where] + part * fade) * gates[span, where]
+                        mix[i, :, where] = value
+                        squares = value * value if squares is None else squares + value * value
+                if j == 0:
+                    sums[i] = squares
+                else:
+                    sums[i] += squares
         for i in range(events // tall):
-            span = pl.ds(pl.multiple_of(u * events + i * tall, tall), tall)
-            squares = None
-            for p in range(0, heads, 2):
-                far = jnp.dot(
-                    outward[span, :],
-                    jnp.concatenate(
-                        [enter[u * per + e // rows, e % rows] for e in (p, p + 1)], axis=1
-                    ),
-                    preferred_element_type=F32,
-                )
-                for e in (p, p + 1):
-                    h = head_of(e)
-                    where = slice(h * LANES, (h + 1) * LANES)
-                    part = far[:, (e - p) * LANES : (e - p + 1) * LANES]
-                    fade = facts[span, 3 * heads + e : 3 * heads + e + 1]
-                    value = (y[span, where] + part * fade) * gates[span, where]
-                    mix[i, :, where] = value
-                    squares = value * value if squares is None else squares + value * value
-            mean = jnp.sum(squares, axis=1, keepdims=True) * (1.0 / inner)
+            span = rows_of(i)
+            mean = jnp.sum(sums[i], axis=1, keepdims=True) * (1.0 / inner)
             normed = (mix[i] * lax.rsqrt(mean + 1.0) * gain_ref[...]).astype(BF16)
             result = jnp.dot(normed, wout[...], preferred_element_type=F32)
             out_ref[span, :] = (result * facts[span, 4 * heads : 4 * heads + 1]).astype(BF16)
@@ -533,7 +600,17 @@
         @pl.when(c < cols - 1)
         def _():
             for k in range(pieces):
-                onward_copy(k).wait_send()
+                near_copy(k).wait_send()
+
+        @pl.when(gives_own)
+        def _():
+            for k in range(pieces):
+                fade_copy(k).wait_send()
+
+        @pl.when(gives_far)
+        def _():
+            for k in range(pieces):
+                far_copy(k).wait_send()
 
 
 def per_device(
@@ -614,14 +691,20 @@
             bf16(pieces, rows, *head),
             f32(users, rows, per, 8, LANES),
             f32(users, rows, per, 8, LANES),
-            f32(rows, *head),
+            f32(pieces, rows + 1, *head),
+            f32(pieces, rows + 1, 8, LANES),
+            f32(*head),
             bf16(pieces, *head),
             bf16(pieces, *head),
+            f32(pieces, 8, LANES),
+            bf16(pieces, *head),
+            f32(pieces, 8, LANES),
             bf16(pieces, rows, *head),
             bf16(pieces, rows, *head),
             f32(total, inner),
             f32(total, inner),
             f32(events // tall, tall, inner),
+            f32(events // tall, tall, LANES),
             pltpu.VMEM((users, 1, STRETCH), jnp.int32),
             dma((heads + 5,)),
             dma((8,)),
@@ -634,6 +717,10 @@
             dma((pieces,)),
             dma((pieces, rows)),
             dma((pieces, rows)),
+            dma((pieces,)),
+            dma((pieces,)),
+            dma((pieces,)),
+            dma((pieces,)),
         ],
         compiler_params=pltpu.CompilerParams(
             collective_id=0, has_side_effects=True, vmem_limit_bytes=48 * 1024 * 1024

time: 35.6 us -> 33.6 us (0.944)
  Pallas kernels: 34.2 us -> 31.8 us
    pallas_call x1, Pallas kernels: 34.2 us -> 31.8 us  [per_device(): pl.pallas_call(functools.partial(mixer_kernel, (rows, cols, users, heads,...]
where the time goes in v3:
time: 33.6 us; the launch traced here: 33.2 us
  Pallas kernels  31.8 us (95%)
  local copies, waits for them, and re-layouts  1.32 us (4%)
    pallas_call x1, Pallas kernels, per_device(): pl.pallas_call(functools.partial(mixer_kernel, (rows, cols, users, heads,...  31.8 us
    unnamed x1, local copies, waits for them, and re-layouts  1.32 us

profile of v3, /device:TPU:24, one launch (start us, length us, event | category | flops | bytes accessed | tf_op | source)
XLA Modules:
  0.0 33.2 jit_solution(17706320673441774166)
XLA Ops:
  0.0 31.8 %mixer.1 = bf16[1024,1024]{1,0:T(8,128)(2,1)S(1)} custom-call(s32[2]{0:T(128)} %lengths_hbm.1, s32[2,1,512]{2,1,0:T(1,128)} %ids_hbm.1, s32[2,1,512]{2,1,0:T(1,128)} %masks_hbm.1, bf16[8,1024]{1,0:T(8,128)(2,1)} %bitcast.8, f32[4,1280]{1,0:T(4,128)} %taps_hbm.1, f32[1,8]{1,0:T(1,128)} %bitcast.10, f32[1,8]{1,0:T(1,128)} %bitcast.11, f32[1,1024]{1,0:T(1,128)} %bitcast.9, ...), custom_call_target="tpu_custom_call" | custom-call | tf_op jit(solution)/shard_map/mixer/pallas_call | solution.py:655
  31.9 1.3 %copy.15 = bf16[2,1,512,1024]{3,2,1,0:T(8,128)(2,1)} copy(bf16[2,1,512,1024]{3,2,1,0:T(8,128)(2,1)S(1)} %bitcast.7) | data formatting | bytes 4194304

commit v4 on v3

--- a/solution.py
+++ b/solution.py
@@ -15,8 +15,8 @@
 BF16 = jnp.bfloat16
 
 
-def silu(v):
-    return 0.5 * v * (1.0 + jnp.tanh(0.5 * v))
+def silu_of_twice(half):
+    return half * (1.0 + jnp.tanh(half))
 
 
 def remote(src, dst, send, recv, device):
@@ -92,6 +92,7 @@
     gates,
     mix,
     sums,
+    partial,
     landed,
     wsem,
     psem,
@@ -109,13 +110,14 @@
     s5,
     r5,
 ):
-    rows, cols, users, heads, tall = counts
+    rows, cols, users, heads, tall, parts = counts
     events = ids_ref.shape[2]
     stretches = events // STRETCH
     kernel = taps_ref.shape[0]
     inner = wgate.shape[1]
     per = heads // rows
-    pieces = users * per
+    pieces = users * per * parts
+    piece_rows = nearin.shape[1]
     wide_group = rows * LANES
     r, c = lax.axis_index("row"), lax.axis_index("col")
     place = c * rows + r
@@ -131,18 +133,23 @@
     def head_of(p):
         return (p % rows) * per + p // rows
 
-    def column(p):
-        source = head_of(p) if not isinstance(p, int) or p < heads else p
-        return pltpu.make_async_copy(
-            win_hbm.at[:, pl.ds(source * LANES, LANES)],
-            win.at[:, pl.ds(p * LANES, LANES)],
-            wsem.at[p],
-        )
+    win_parts = 4
+    win_rows = win.shape[0] // win_parts
+
+    def win_copy(i):
+        lines = pl.ds(i * win_rows, win_rows)
+        return pltpu.make_async_copy(win_hbm.at[lines, :], win.at[lines, :], wsem.at[i])
 
     blocks = heads + 2
     table_copy = pltpu.make_async_copy(table_hbm, table, wsem.at[blocks])
     wgate_copy = pltpu.make_async_copy(wgate_hbm, wgate, wsem.at[blocks + 1])
-    wout_copy = pltpu.make_async_copy(wout_hbm, wout, wsem.at[blocks + 2])
+
+    def wout_copy(p):
+        return pltpu.make_async_copy(
+            wout_hbm.at[pl.ds(head_of(p) * LANES, LANES), :],
+            wout.at[pl.ds(p * LANES, LANES), :],
+            wsem.at[blocks + 2 + p],
+        )
     small = [
         pltpu.make_async_copy(source, target, psem.at[i])
         for i, (source, target) in enumerate(
@@ -158,11 +165,11 @@
             )
         )
     ]
-    table_copy.start()
     for copy in small:
         copy.start()
-    for p in (heads, heads + 1, *range(heads)):
-        column(p).start()
+    table_copy.start()
+    for i in range(win_parts):
+        win_copy(i).start()
 
     barrier = pltpu.get_barrier_semaphore()
     for d in range(1, rows):
@@ -201,6 +208,22 @@
     wide[...] = jnp.zeros_like(wide)
     for copy in small:
         copy.wait()
+    peers = (
+        rows
+        - 1
+        + jnp.where(c > 0, 1, 0)
+        + jnp.where(c < cols - 1, 1, 0)
+        + jnp.where(c > 1, 1, 0)
+        + jnp.where(c < cols - 2, 1, 0)
+        + jnp.where(wraps, 1, 0)
+        + jnp.where(wrapped, 1, 0)
+    )
+    pl.semaphore_wait(barrier, peers)
+
+    @pl.when(has_after)
+    def _():
+        halo_copy.start()
+
     line_rows = lax.broadcasted_iota(jnp.int32, (STRETCH, STRETCH), 0)
     line_cols = lax.broadcasted_iota(jnp.int32, (STRETCH, STRETCH), 1)
     causal = line_rows >= line_cols
@@ -214,53 +237,45 @@
     )
     for p in range(blocks):
         source = p if p >= heads else head_of(p)
-        ptaps[p, 0:kernel, :] = taps_ref[:, source * LANES : (source + 1) * LANES]
+        scale = 0.5 if p < heads else 1.0
+        ptaps[p, 0:kernel, :] = scale * taps_ref[:, source * LANES : (source + 1) * LANES]
 
     table_copy.wait()
 
-    def table_block(first):
-        span = pl.ds(first, 2 * LANES)
-        if not isinstance(first, int):
-            span = pl.ds(pl.multiple_of(first, 2 * LANES), 2 * LANES)
-        tin[:, span] = jnp.dot(table[...], win[:, span], preferred_element_type=F32).astype(BF16)
-
-    column(heads).wait()
-    column(heads + 1).wait()
-    table_block(heads * LANES)
+    for i in range(win_parts):
+        win_copy(i).wait()
+
+    def table_pair(first, left, right):
+        weights = jnp.concatenate([win[:, left], win[:, right]], axis=1)
+        tin[:, pl.ds(first, 2 * LANES)] = jnp.dot(
+            table[...], weights, preferred_element_type=F32
+        ).astype(BF16)
+
+    table_pair(
+        heads * LANES,
+        slice(heads * LANES, (heads + 1) * LANES),
+        slice((heads + 1) * LANES, (heads + 2) * LANES),
+    )
 
     raw = lax.dot_general(
-        table[...], wide[...], (((1,), (1,)), ((), ())), preferred_element_type=F32
-    )
+        wide[...], table[...], (((1,), (1,)), ((), ())), preferred_element_type=F32
+    )[0:heads]
     high = raw.astype(BF16).astype(F32)
     middle = (raw - high).astype(BF16).astype(F32)
     low = raw - high - middle
-    tdt[...] = (high + pltpu.roll(middle, heads, 1) + pltpu.roll(low, 2 * heads, 1)).astype(BF16)
-
-    peers = (
-        rows
-        - 1
-        + jnp.where(c > 0, 1, 0)
-        + jnp.where(c < cols - 1, 1, 0)
-        + jnp.where(c > 1, 1, 0)
-        + jnp.where(c < cols - 2, 1, 0)
-        + jnp.where(wraps, 1, 0)
-        + jnp.where(wrapped, 1, 0)
-    )
-    pl.semaphore_wait(barrier, peers)
-
-    @pl.when(has_after)
-    def _():
-        halo_copy.start()
+    tdt[...] = jnp.concatenate([high, middle, low, jnp.zeros_like(low)], axis=0).astype(BF16)
 
     def table_step(i, carry):
-        column(2 * i).wait()
-        column(2 * i + 1).wait()
-        table_block(i * 2 * LANES)
+        left, right = (
+            pl.ds(pl.multiple_of(head_of(2 * i + e) * LANES, LANES), LANES) for e in (0, 1)
+        )
+        table_pair(pl.multiple_of(i * 2 * LANES, 2 * LANES), left, right)
         return carry
 
     lax.fori_loop(0, heads // 2, table_step, 0)
     wgate_copy.start()
-    wout_copy.start()
+    for p in range(heads):
+        wout_copy(p).start()
 
     @pl.when(place == 0)
     def _():
@@ -270,10 +285,10 @@
     def _():
         halo_copy.wait_recv()
 
-    def convolve(position, slot):
+    def convolve(position):
         total = None
         for k in range(kernel):
-            part = rowbuf[slot, pl.ds(HALO - kernel + 1 + k, events), :] * ptaps[position, k : k + 1, :]
+            part = rowbuf[position, pl.ds(HALO - kernel + 1 + k, events), :] * ptaps[position, k : k + 1, :]
             total = part if total is None else total + part
         return total
 
@@ -319,12 +334,15 @@
         items = table.shape[0]
         lane = lax.broadcasted_iota(jnp.int32, (HALO + events, items), 1)
         hot[u] = (ids == lane).astype(F32).astype(BF16)
-        both = jnp.dot(hot[u], tin[:, heads * LANES :], preferred_element_type=F32)
-        rowbuf[0] = both[:, :LANES]
-        rowbuf[1] = both[:, LANES:]
-        parts = jnp.dot(hot[u, pl.ds(HALO, events), :], tdt[...], preferred_element_type=F32)
-        parts = jnp.transpose(parts)
-        raw = parts[0:heads] + parts[heads : 2 * heads] + parts[2 * heads : 3 * heads]
+        shares = lax.dot_general(
+            tdt[...],
+            hot[u, pl.ds(HALO, events), :],
+            (((1,), (1,)), ((), ())),
+            preferred_element_type=F32,
+        )
+        gather_pair(u, heads // 2)
+        gather_pair(u, 0)
+        raw = shares[0:heads] + shares[heads : 2 * heads] + shares[2 * heads : 3 * heads]
         upper = jnp.where(line_rows <= line_cols, 1.0, 0.0).astype(F32)
         steps, paced = [], []
         for s in range(stretches):
@@ -363,33 +381,35 @@
             past = past + total
         for p in range(heads):
             aft[u, p % rows, p // rows] = jnp.broadcast_to(past[p : p + 1], (8, LANES))
-        inward_t[u] = jnp.transpose(convolve(heads, 0)).astype(BF16)
-        outward[pl.ds(pl.multiple_of(u * events, events), events), :] = convolve(heads + 1, 1).astype(BF16)
+        inward_t[u] = jnp.transpose(convolve(heads)).astype(BF16)
+        outward[pl.ds(pl.multiple_of(u * events, events), events), :] = convolve(heads + 1).astype(BF16)
         for d in range(1, rows):
             log_copy(u, d).start()
         lin[u, r] = aft[u, r]
 
-    def group(u, j):
+    def gather_pair(u, a):
+        both = jnp.dot(
+            hot[u], tin[:, 2 * a * LANES : 2 * (a + 1) * LANES], preferred_element_type=F32
+        )
+        rowbuf[2 * a] = both[:, :LANES]
+        rowbuf[2 * a + 1] = both[:, LANES:]
+
+    def convert(u, p):
+        mine = pl.ds(pl.multiple_of(u * events, events), events)
+        j, q = p // rows, p % rows
+        value = silu_of_twice(convolve(p)).astype(BF16)
+        signal[u, p] = value
+        scaled[j, :, q * LANES : (q + 1) * LANES] = (
+            value.astype(F32) * facts[mine, heads + p : heads + p + 1]
+        ).astype(BF16)
+
+    def form_state(u, j):
         k = u * per + j
-        mine = pl.ds(pl.multiple_of(u * events, events), events)
-        gathered = jnp.dot(
-            hot[u], tin[:, j * wide_group : (j + 1) * wide_group], preferred_element_type=F32
-        )
-        for q in range(rows):
-            rowbuf[q] = gathered[:, q * LANES : (q + 1) * LANES]
-        for q in range(rows):
-            span = slice(q * LANES, (q + 1) * LANES)
-            value = silu(convolve(j * rows + q, q)).astype(BF16)
-            signal[u, j * rows + q] = value
-            scaled[:, span] = (
-                value.astype(F32)
-                * facts[mine, heads + j * rows + q : heads + j * rows + q + 1]
-            ).astype(BF16)
         run = None
         for s in range(stretches):
             span = slice(s * STRETCH, (s + 1) * STRETCH)
             added = jnp.dot(
-                inward_t[u, :, span], scaled[span, :], preferred_element_type=F32
+                inward_t[u, :, span], scaled[j, span, :], preferred_element_type=F32
             )
             if run is None:
                 held[k, s] = jnp.zeros_like(held[k, s])
@@ -397,15 +417,23 @@
             else:
                 held[k, s] = run.astype(BF16)
                 run = run * shrinks[k, s, 0:1, :] + added
-        for q in range(rows):
-            ssend[k, q] = run[:, q * LANES : (q + 1) * LANES].astype(BF16)
-        for d in range(1, rows):
-            state_copy(k, d).start()
+        for i in range(parts):
+            lines = slice(i * piece_rows, (i + 1) * piece_rows)
+            for q in range(rows):
+                ssend[k * parts + i, q] = run[lines, q * LANES : (q + 1) * LANES].astype(BF16)
+            for d in range(1, rows):
+                state_copy(k * parts + i, d).start()
 
     def user_step(u, carry):
         prepare(u)
-        for j in range(per):
-            group(u, j)
+        for a in range(heads // 2):
+            if a + 1 < heads // 2:
+                gather_pair(u, a + 1)
+            convert(u, 2 * a)
+            convert(u, 2 * a + 1)
+            for j in range(per):
+                if 2 * a < (j + 1) * rows <= 2 * a + 2:
+                    form_state(u, j)
         return carry
 
     lax.fori_loop(0, users, user_step, 0)
@@ -417,10 +445,10 @@
     takes_far = jnp.logical_and(odd, c > 1)
 
     def gather_piece(k, carry):
-        u, j = k // per, lax.rem(k, per)
+        u, j = k // (per * parts), lax.rem(k // parts, per)
         rin[k, r] = ssend[k, r]
 
-        @pl.when(j == 0)
+        @pl.when(lax.rem(k, per * parts) == 0)
         def _():
             for d in range(1, rows):
                 log_copy(u, d).wait_recv()
@@ -472,11 +500,14 @@
             @pl.when(gives_near)
             def _():
                 psend[k] = (fades[k, rows, 0:1] * pin[...] + before[k, rows]).astype(BF16)
-                near_copy(k).start()
 
             @pl.when(gives_far)
             def _():
                 far_copy(k).start()
+
+            @pl.when(gives_near)
+            def _():
+                near_copy(k).start()
 
         for q in range(rows):
             esend[k, q] = (fades[k, q, 0:1] * pin[...] + before[k, q]).astype(BF16)
@@ -488,7 +519,9 @@
     ticks = users * stretches
 
     def due(t):
-        return jnp.minimum(jnp.maximum(t, 0) // 2, pieces)
+        t = jnp.maximum(t, -1) + stretches
+        whole, rest = t // stretches - 1, lax.rem(t, stretches)
+        return jnp.minimum(jnp.maximum(whole * per + jnp.minimum(rest + 1, per), 0) * parts, pieces)
 
     lag = jnp.where(c == 0, 0, 4 * ((c + 2) // 2))
 
@@ -496,7 +529,7 @@
     chunk = inner // stretches
 
     def local_step(t, done):
-        now = due(t + 1), due(t + 1 - lag)
+        now = due(t), due(t - lag)
         lax.fori_loop(done[0], now[0], gather_piece, 0)
         lax.fori_loop(done[1], now[1], enter_piece, 0)
         u, s = t // stretches, lax.rem(t, stretches)
@@ -505,11 +538,11 @@
 
         @pl.when(u == 0)
         def _():
-            tgate[:, span] = jnp.dot(
-                table[...], wgate[:, span], preferred_element_type=F32
+            tgate[:, span] = (
+                0.5 * jnp.dot(table[...], wgate[:, span], preferred_element_type=F32)
             ).astype(BF16)
 
-        gates[mine, span] = silu(
+        gates[mine, span] = silu_of_twice(
             jnp.dot(hot[u, pl.ds(HALO, events), :], tgate[:, span], preferred_element_type=F32)
         )
         base = pl.multiple_of(s * STRETCH, STRETCH)
@@ -542,23 +575,30 @@
     done = lax.fori_loop(0, ticks, local_step, (0, 0))
     lax.fori_loop(done[0], pieces, gather_piece, 0)
     lax.fori_loop(done[1], pieces, enter_piece, 0)
-    wout_copy.wait()
+    for p in range(heads):
+        wout_copy(p).wait()
 
     def finish_step(u, carry):
         def rows_of(i):
             return pl.ds(pl.multiple_of(u * events + i * tall, tall), tall)
 
         for j in range(per):
-            for d in range(1, rows):
-                enter_copy(u * per + j, d).wait_recv()
+            base = (u * per + j) * parts
+            for i in range(parts):
+                for d in range(1, rows):
+                    enter_copy(base + i, d).wait_recv()
             for i in range(events // tall):
                 span = rows_of(i)
                 squares = None
                 for q in range(0, rows, 2):
                     pair = range(q, min(q + 2, rows))
+                    state = [
+                        jnp.concatenate([enter[base + n, e] for n in range(parts)], axis=0)
+                        for e in pair
+                    ]
                     far = jnp.dot(
                         outward[span, :],
-                        jnp.concatenate([enter[u * per + j, e] for e in pair], axis=1),
+                        jnp.concatenate(state, axis=1),
                         preferred_element_type=F32,
                     )
                     for e in pair:
@@ -568,18 +608,23 @@
                         part = far[:, (e - q) * LANES : (e - q + 1) * LANES]
                         fade = facts[span, 3 * heads + p : 3 * heads + p + 1]
                         value = (y[span, where] + part * fade) * gates[span, where]
-                        mix[i, :, where] = value
+                        mix[i, :, e * LANES : (e + 1) * LANES] = (value * gain_ref[:, where]).astype(BF16)
                         squares = value * value if squares is None else squares + value * value
-                if j == 0:
+                product = jnp.dot(
+                    mix[i],
+                    wout[j * wide_group : (j + 1) * wide_group, :],
+                    preferred_element_type=F32,
+                )
+                if j > 0:
+                    squares = squares + sums[i]
+                    product = product + partial[i]
+                if j < per - 1:
                     sums[i] = squares
+                    partial[i] = product
                 else:
-                    sums[i] += squares
-        for i in range(events // tall):
-            span = rows_of(i)
-            mean = jnp.sum(sums[i], axis=1, keepdims=True) * (1.0 / inner)
-            normed = (mix[i] * lax.rsqrt(mean + 1.0) * gain_ref[...]).astype(BF16)
-            result = jnp.dot(normed, wout[...], preferred_element_type=F32)
-            out_ref[span, :] = (result * facts[span, 4 * heads : 4 * heads + 1]).astype(BF16)
+                    mean = jnp.sum(squares, axis=1, keepdims=True) * (1.0 / inner)
+                    scale = lax.rsqrt(mean + 1.0) * facts[span, 4 * heads : 4 * heads + 1]
+                    out_ref[span, :] = (product * scale).astype(BF16)
         return carry
 
     lax.fori_loop(0, users, finish_step, 0)
@@ -636,11 +681,12 @@
     rows, cols = lax.axis_size("row"), lax.axis_size("col")
     stretches = events // STRETCH
     per = heads // rows
-    pieces = users * per
+    parts = 1
+    pieces = users * per * parts
     total = users * events
     tall = 2 * STRETCH if events % (2 * STRETCH) == 0 else STRETCH
     group = rows * LANES
-    head = (state_width, LANES)
+    head = (state_width // parts, LANES)
 
     vmem = pl.BlockSpec(memory_space=pltpu.VMEM)
     hbm = pl.BlockSpec(memory_space=pltpu.HBM)
@@ -653,7 +699,7 @@
         return pltpu.VMEM(shape, BF16)
 
     result = pl.pallas_call(
-        functools.partial(mixer_kernel, (rows, cols, users, heads, tall)),
+        functools.partial(mixer_kernel, (rows, cols, users, heads, tall, parts)),
         in_specs=[hbm] * 12,
         out_specs=vmem,
         out_shape=jax.ShapeDtypeStruct((total, w_out.shape[1]), BF16),
@@ -672,21 +718,21 @@
             bf16(*w_out.shape),
             bf16(items, full_width),
             bf16(items, inner),
-            bf16(items, LANES),
-            bf16(LANES, model),
+            bf16(4 * heads, items),
+            bf16(2 * heads, model),
             f32(2, heads, LANES),
             f32(heads + 2, 8, LANES),
             bf16(users, HALO + events, items),
-            f32(max(rows, 2), HALO + events, LANES),
+            f32(heads + 2, HALO + events, LANES),
             bf16(users, state_width, events),
             bf16(total, state_width),
             f32(total, LANES),
             f32(users, stretches, heads, LANES),
             f32(users, stretches, heads, LANES),
-            f32(pieces, stretches, 8, group),
+            f32(users * per, stretches, 8, group),
             bf16(users, heads, events, LANES),
-            bf16(events, group),
-            bf16(pieces, stretches, state_width, group),
+            bf16(per, events, group),
+            bf16(users * per, stretches, state_width, group),
             bf16(pieces, rows, *head),
             bf16(pieces, rows, *head),
             f32(users, rows, per, 8, LANES),
@@ -703,10 +749,11 @@
             bf16(pieces, rows, *head),
             f32(total, inner),
             f32(total, inner),
-            f32(events // tall, tall, inner),
+            bf16(events // tall, tall, group),
             f32(events // tall, tall, LANES),
+            f32(events // tall, tall, w_out.shape[1]),
             pltpu.VMEM((users, 1, STRETCH), jnp.int32),
-            dma((heads + 5,)),
+            dma((2 * heads + 4,)),
             dma((8,)),
             dma((2,)),
             dma((users, rows)),

time: 33.6 us -> 31.1 us (0.926)
  Pallas kernels: 31.8 us -> 29.2 us
    pallas_call x1, Pallas kernels: 31.8 us -> 29.2 us  [per_device(): pl.pallas_call(functools.partial(mixer_kernel, (rows, cols, users, heads,...]
where the time goes in v4:
time: 31.1 us; the launch traced here: 30.5 us
  Pallas kernels  29.2 us (94%)
  local copies, waits for them, and re-layouts  1.32 us (4%)
    pallas_call x1, Pallas kernels, per_device(): pl.pallas_call(functools.partial(mixer_kernel, (rows, cols, users, heads,...  29.2 us
    unnamed x1, local copies, waits for them, and re-layouts  1.32 us

profile of v4, /device:TPU:24, one launch (start us, length us, event | category | flops | bytes accessed | tf_op | source)
XLA Modules:
  0.0 30.5 jit_solution(6545907368817593863)
XLA Ops:
  0.0 29.2 %mixer.1 = bf16[1024,1024]{1,0:T(8,128)(2,1)S(1)} custom-call(s32[2]{0:T(128)} %lengths_hbm.1, s32[2,1,512]{2,1,0:T(1,128)} %ids_hbm.1, s32[2,1,512]{2,1,0:T(1,128)} %masks_hbm.1, bf16[8,1024]{1,0:T(8,128)(2,1)} %bitcast.8, f32[4,1280]{1,0:T(4,128)} %taps_hbm.1, f32[1,8]{1,0:T(1,128)} %bitcast.10, f32[1,8]{1,0:T(1,128)} %bitcast.11, f32[1,1024]{1,0:T(1,128)} %bitcast.9, ...), custom_call_target="tpu_custom_call" | custom-call | tf_op jit(solution)/shard_map/mixer/pallas_call | solution.py:701
  29.2 1.3 %copy.15 = bf16[2,1,512,1024]{3,2,1,0:T(8,128)(2,1)} copy(bf16[2,1,512,1024]{3,2,1,0:T(8,128)(2,1)S(1)} %bitcast.7) | data formatting | bytes 4194304

commit v5 on v4

--- a/solution.py
+++ b/solution.py
@@ -85,6 +85,7 @@
     farin,
     fadein,
     psend,
+    qsend,
     fsend,
     esend,
     enter,
@@ -208,6 +209,18 @@
     wide[...] = jnp.zeros_like(wide)
     for copy in small:
         copy.wait()
+    def mark_items(u, ids, skip, first, count):
+        names = jnp.transpose(jnp.broadcast_to(ids.astype(F32), (8, ids.shape[1])))
+        names = names[skip:, 0:1].astype(jnp.int32)
+        lane = lax.broadcasted_iota(jnp.int32, (count, table.shape[0]), 1)
+        hot[u, first : first + count, :] = (names == lane).astype(F32).astype(BF16)
+
+    def mark_step(u, carry):
+        mark_items(u, ids_ref[u], 0, HALO, events)
+        return carry
+
+    lax.fori_loop(0, users, mark_step, 0)
+
     peers = (
         rows
         - 1
@@ -265,14 +278,14 @@
     low = raw - high - middle
     tdt[...] = jnp.concatenate([high, middle, low, jnp.zeros_like(low)], axis=0).astype(BF16)
 
-    def table_step(i, carry):
-        left, right = (
-            pl.ds(pl.multiple_of(head_of(2 * i + e) * LANES, LANES), LANES) for e in (0, 1)
-        )
-        table_pair(pl.multiple_of(i * 2 * LANES, 2 * LANES), left, right)
-        return carry
-
-    lax.fori_loop(0, heads // 2, table_step, 0)
+    for i in range(heads // 2):
+        table_pair(
+            i * 2 * LANES,
+            *(
+                slice(head_of(p) * LANES, (head_of(p) + 1) * LANES)
+                for p in (2 * i, 2 * i + 1)
+            ),
+        )
     wgate_copy.start()
     for p in range(heads):
         wout_copy(p).start()
@@ -314,7 +327,7 @@
 
     def far_copy(k):
         return remote(
-            psend.at[k], farin.at[k], s5.at[k], r5.at[k], {"col": lax.rem(c + 2, cols)}
+            qsend.at[k], farin.at[k], s5.at[k], r5.at[k], {"col": lax.rem(c + 2, cols)}
         )
 
     def enter_copy(k, d):
@@ -323,17 +336,10 @@
 
     def prepare(u):
         first = place * events
-        names = jnp.concatenate([landed[u], ids_ref[u]], axis=1).astype(F32)
         position = first + lax.broadcasted_iota(jnp.int32, (1, events), 1)
         kept = jnp.where(position < lengths_ref[u], masks_ref[u], 0)
         kept = jnp.where(kept > 0, 1.0, 0.0).astype(F32)
-        flags = jnp.concatenate([jnp.zeros((1, STRETCH), F32), kept], axis=1)
-        line = lax.broadcasted_iota(jnp.int32, (8, STRETCH + events), 0)
-        meta = jnp.transpose(jnp.where(line == 0, names, jnp.where(line == 1, flags, 0.0)))
-        ids = meta[STRETCH - HALO :, 0:1].astype(jnp.int32)
-        items = table.shape[0]
-        lane = lax.broadcasted_iota(jnp.int32, (HALO + events, items), 1)
-        hot[u] = (ids == lane).astype(F32).astype(BF16)
+        mark_items(u, landed[u], STRETCH - HALO, 0, HALO)
         shares = lax.dot_general(
             tdt[...],
             hot[u, pl.ds(HALO, events), :],
@@ -438,11 +444,8 @@
 
     lax.fori_loop(0, users, user_step, 0)
 
-    odd = lax.rem(c, 2) == 1
-    gives_own = jnp.logical_and(jnp.logical_not(odd), c < cols - 1)
-    gives_near = jnp.logical_and(odd, c < cols - 1)
-    gives_far = jnp.logical_and(odd, c < cols - 2)
-    takes_far = jnp.logical_and(odd, c > 1)
+    gives_near = c < cols - 1
+    gives_far = c < cols - 2
 
     def gather_piece(k, carry):
         u, j = k // (per * parts), lax.rem(k // parts, per)
@@ -467,7 +470,7 @@
         fades[k, rows] = fade
         if cols > 1:
 
-            @pl.when(gives_own)
+            @pl.when(gives_near)
             def _():
                 psend[k] = carried.astype(BF16)
                 fsend[k] = fade
@@ -486,28 +489,18 @@
             @pl.when(c > 0)
             def _():
                 near_copy(k).wait_recv()
+                fade_copy(k).wait_recv()
                 pin[...] = nearin[k].astype(F32)
 
-            @pl.when(odd)
-            def _():
-                fade_copy(k).wait_recv()
-
-            @pl.when(takes_far)
+            @pl.when(c > 1)
             def _():
                 far_copy(k).wait_recv()
                 pin[...] = fadein[k, 0:1] * farin[k].astype(F32) + nearin[k].astype(F32)
 
-            @pl.when(gives_near)
-            def _():
-                psend[k] = (fades[k, rows, 0:1] * pin[...] + before[k, rows]).astype(BF16)
-
             @pl.when(gives_far)
             def _():
+                qsend[k] = (fades[k, rows, 0:1] * pin[...] + before[k, rows]).astype(BF16)
                 far_copy(k).start()
-
-            @pl.when(gives_near)
-            def _():
-                near_copy(k).start()
 
         for q in range(rows):
             esend[k, q] = (fades[k, q, 0:1] * pin[...] + before[k, q]).astype(BF16)
@@ -518,12 +511,12 @@
 
     ticks = users * stretches
 
+    marks = [u * stretches + (j if u == 0 else 0) for u in range(users) for j in range(per)]
+
     def due(t):
-        t = jnp.maximum(t, -1) + stretches
-        whole, rest = t // stretches - 1, lax.rem(t, stretches)
-        return jnp.minimum(jnp.maximum(whole * per + jnp.minimum(rest + 1, per), 0) * parts, pieces)
-
-    lag = jnp.where(c == 0, 0, 4 * ((c + 2) // 2))
+        return sum(jnp.where(t >= mark, 1, 0) for mark in marks)
+
+    lag = jnp.maximum(2 * c - 1, 0)
 
     wgate_copy.wait()
     chunk = inner // stretches
@@ -642,14 +635,10 @@
             enter_copy(k, d).wait_send()
     if cols > 1:
 
-        @pl.when(c < cols - 1)
+        @pl.when(gives_near)
         def _():
             for k in range(pieces):
                 near_copy(k).wait_send()
-
-        @pl.when(gives_own)
-        def _():
-            for k in range(pieces):
                 fade_copy(k).wait_send()
 
         @pl.when(gives_far)
@@ -743,6 +732,7 @@
             bf16(pieces, *head),
             bf16(pieces, *head),
             f32(pieces, 8, LANES),
+            bf16(pieces, *head),
             bf16(pieces, *head),
             f32(pieces, 8, LANES),
             bf16(pieces, rows, *head),

time: 31.1 us -> 29.9 us (0.961); the launches traced: 30.5 us -> 29.7 us
  Pallas kernels: 29.2 us -> 28.4 us
    pallas_call x1, Pallas kernels: 29.2 us -> 28.4 us  [per_device(): pl.pallas_call(functools.partial(mixer_kernel, (rows, cols, users, heads,...]
where the time goes in v5:
time: 29.9 us; the launch traced here: 29.7 us
  Pallas kernels  28.4 us (95%)
  local copies, waits for them, and re-layouts  1.32 us (4%)
    pallas_call x1, Pallas kernels, per_device(): pl.pallas_call(functools.partial(mixer_kernel, (rows, cols, users, heads,...  28.4 us
    unnamed x1, local copies, waits for them, and re-layouts  1.32 us

profile of v5, /device:TPU:24, one launch (start us, length us, event | category | flops | bytes accessed | tf_op | source)
XLA Modules:
  0.0 29.7 jit_solution(15140220374343059060)
XLA Ops:
  0.0 28.4 %mixer.1 = bf16[1024,1024]{1,0:T(8,128)(2,1)S(1)} custom-call(s32[2]{0:T(128)} %lengths_hbm.1, s32[2,1,512]{2,1,0:T(1,128)} %ids_hbm.1, s32[2,1,512]{2,1,0:T(1,128)} %masks_hbm.1, bf16[8,1024]{1,0:T(8,128)(2,1)} %bitcast.8, f32[4,1280]{1,0:T(4,128)} %taps_hbm.1, f32[1,8]{1,0:T(1,128)} %bitcast.10, f32[1,8]{1,0:T(1,128)} %bitcast.11, f32[1,1024]{1,0:T(1,128)} %bitcast.9, ...), custom_call_target="tpu_custom_call" | custom-call | tf_op jit(solution)/shard_map/mixer/pallas_call | solution.py:690
  28.4 1.3 %copy.15 = bf16[2,1,512,1024]{3,2,1,0:T(8,128)(2,1)} copy(bf16[2,1,512,1024]{3,2,1,0:T(8,128)(2,1)S(1)} %bitcast.7) | data formatting | bytes 4194304

commit v6 on v5

--- a/solution.py
+++ b/solution.py
@@ -298,12 +298,20 @@
     def _():
         halo_copy.wait_recv()
 
-    def convolve(position):
+    def own_rows(u):
+        first = u * events
+        return pl.ds(first if isinstance(u, int) else pl.multiple_of(first, events), events)
+
+    def convolve(u, position):
         total = None
         for k in range(kernel):
-            part = rowbuf[position, pl.ds(HALO - kernel + 1 + k, events), :] * ptaps[position, k : k + 1, :]
+            part = rowbuf[u, position, pl.ds(HALO - kernel + 1 + k, events), :] * ptaps[position, k : k + 1, :]
             total = part if total is None else total + part
         return total
+
+    even = lax.rem(r, 2) == 0
+    ends = [jnp.where(even, rows - 1, 1), jnp.where(even, 1, rows - 1)]
+    sending_order = [ends[0], *range(2, rows - 1), ends[1]] if rows > 2 else [*range(1, rows)]
 
     def log_copy(u, d):
         q = lax.rem(r + d, rows)
@@ -377,7 +385,7 @@
                     jnp.broadcast_to(shrink[p : p + 1], (8, LANES))
                 )
             used = jnp.broadcast_to(kept[:, s * STRETCH : (s + 1) * STRETCH], (heads, LANES))
-            facts[pl.ds(pl.multiple_of(u * events + s * STRETCH, STRETCH), STRETCH), :] = jnp.transpose(
+            facts[pl.ds(u * events + s * STRETCH, STRETCH), :] = jnp.transpose(
                 jnp.concatenate(
                     [log, tail, jnp.exp(-log), jnp.exp(-(log + past)), used]
                     + [jnp.zeros((LANES - 5 * heads, LANES), F32)],
@@ -387,8 +395,8 @@
             past = past + total
         for p in range(heads):
             aft[u, p % rows, p // rows] = jnp.broadcast_to(past[p : p + 1], (8, LANES))
-        inward_t[u] = jnp.transpose(convolve(heads)).astype(BF16)
-        outward[pl.ds(pl.multiple_of(u * events, events), events), :] = convolve(heads + 1).astype(BF16)
+        inward_t[u] = jnp.transpose(convolve(u, heads)).astype(BF16)
+        outward[own_rows(u), :] = convolve(u, heads + 1).astype(BF16)
         for d in range(1, rows):
             log_copy(u, d).start()
         lin[u, r] = aft[u, r]
@@ -397,15 +405,15 @@
         both = jnp.dot(
             hot[u], tin[:, 2 * a * LANES : 2 * (a + 1) * LANES], preferred_element_type=F32
         )
-        rowbuf[2 * a] = both[:, :LANES]
-        rowbuf[2 * a + 1] = both[:, LANES:]
+        rowbuf[u, 2 * a] = both[:, :LANES]
+        rowbuf[u, 2 * a + 1] = both[:, LANES:]
 
     def convert(u, p):
-        mine = pl.ds(pl.multiple_of(u * events, events), events)
+        mine = own_rows(u)
         j, q = p // rows, p % rows
-        value = silu_of_twice(convolve(p)).astype(BF16)
+        value = silu_of_twice(convolve(u, p)).astype(BF16)
         signal[u, p] = value
-        scaled[j, :, q * LANES : (q + 1) * LANES] = (
+        scaled[u, j, :, q * LANES : (q + 1) * LANES] = (
             value.astype(F32) * facts[mine, heads + p : heads + p + 1]
         ).astype(BF16)
 
@@ -415,7 +423,7 @@
         for s in range(stretches):
             span = slice(s * STRETCH, (s + 1) * STRETCH)
             added = jnp.dot(
-                inward_t[u, :, span], scaled[j, span, :], preferred_element_type=F32
+                inward_t[u, :, span], scaled[u, j, span, :], preferred_element_type=F32
             )
             if run is None:
                 held[k, s] = jnp.zeros_like(held[k, s])
@@ -427,7 +435,7 @@
             lines = slice(i * piece_rows, (i + 1) * piece_rows)
             for q in range(rows):
                 ssend[k * parts + i, q] = run[lines, q * LANES : (q + 1) * LANES].astype(BF16)
-            for d in range(1, rows):
+            for d in sending_order:
                 state_copy(k * parts + i, d).start()
 
     def user_step(u, carry):
@@ -442,7 +450,8 @@
                     form_state(u, j)
         return carry
 
-    lax.fori_loop(0, users, user_step, 0)
+    for u in range(users):
+        user_step(u, 0)
 
     gives_near = c < cols - 1
     gives_far = c < cols - 2
@@ -504,7 +513,7 @@
 
         for q in range(rows):
             esend[k, q] = (fades[k, q, 0:1] * pin[...] + before[k, q]).astype(BF16)
-        for d in range(1, rows):
+        for d in sending_order:
             enter_copy(k, d).start()
         enter[k, r] = esend[k, r]
         return carry
@@ -527,7 +536,7 @@
         lax.fori_loop(done[1], now[1], enter_piece, 0)
         u, s = t // stretches, lax.rem(t, stretches)
         span = pl.ds(pl.multiple_of(s * chunk, chunk), chunk)
-        mine = pl.ds(pl.multiple_of(u * events, events), events)
+        mine = own_rows(u)
 
         @pl.when(u == 0)
         def _():
@@ -712,7 +721,7 @@
             f32(2, heads, LANES),
             f32(heads + 2, 8, LANES),
             bf16(users, HALO + events, items),
-            f32(heads + 2, HALO + events, LANES),
+            f32(users, heads + 2, HALO + events, LANES),
             bf16(users, state_width, events),
             bf16(total, state_width),
             f32(total, LANES),
@@ -720,7 +729,7 @@
             f32(users, stretches, heads, LANES),
             f32(users * per, stretches, 8, group),
             bf16(users, heads, events, LANES),
-            bf16(per, events, group),
+            bf16(users, per, events, group),
             bf16(users * per, stretches, state_width, group),
             bf16(pieces, rows, *head),
             bf16(pieces, rows, *head),

time: 29.9 us -> 29.8 us (level)
  no operation moved by 1% of the time
where the time goes in v6:
time: 29.8 us; the launch traced here: 29.6 us
  Pallas kernels  28.3 us (95%)
  local copies, waits for them, and re-layouts  1.32 us (4%)
    pallas_call x1, Pallas kernels, per_device(): pl.pallas_call(functools.partial(mixer_kernel, (rows, cols, users, heads,...  28.3 us
    unnamed x1, local copies, waits for them, and re-layouts  1.32 us

profile of v6, /device:TPU:24, one launch (start us, length us, event | category | flops | bytes accessed | tf_op | source)
XLA Modules:
  0.0 29.6 jit_solution(14212397165879060822)
XLA Ops:
  0.0 28.3 %mixer.1 = bf16[1024,1024]{1,0:T(8,128)(2,1)S(1)} custom-call(s32[2]{0:T(128)} %lengths_hbm.1, s32[2,1,512]{2,1,0:T(1,128)} %ids_hbm.1, s32[2,1,512]{2,1,0:T(1,128)} %masks_hbm.1, bf16[8,1024]{1,0:T(8,128)(2,1)} %bitcast.8, f32[4,1280]{1,0:T(4,128)} %taps_hbm.1, f32[1,8]{1,0:T(1,128)} %bitcast.10, f32[1,8]{1,0:T(1,128)} %bitcast.11, f32[1,1024]{1,0:T(1,128)} %bitcast.9, ...), custom_call_target="tpu_custom_call" | custom-call | tf_op jit(solution)/shard_map/mixer/pallas_call | solution.py:699
  28.3 1.3 %copy.15 = bf16[2,1,512,1024]{3,2,1,0:T(8,128)(2,1)} copy(bf16[2,1,512,1024]{3,2,1,0:T(8,128)(2,1)S(1)} %bitcast.7) | data formatting | bytes 4194304

commit v7 on v6

--- a/solution.py
+++ b/solution.py
@@ -520,7 +520,7 @@
 
     ticks = users * stretches
 
-    marks = [u * stretches + (j if u == 0 else 0) for u in range(users) for j in range(per)]
+    marks = [u * (stretches - 1) + j for u in range(users) for j in range(per)]
 
     def due(t):
         return sum(jnp.where(t >= mark, 1, 0) for mark in marks)

time: 29.8 us -> 29.4 us (0.987)
  Pallas kernels: 28.3 us -> 27.9 us
    pallas_call x1, Pallas kernels: 28.3 us -> 27.9 us  [per_device(): pl.pallas_call(functools.partial(mixer_kernel, (rows, cols, users, heads,...]
where the time goes in v7:
time: 29.4 us; the launch traced here: 29.2 us
  Pallas kernels  27.9 us (95%)
  local copies, waits for them, and re-layouts  1.32 us (4%)
    pallas_call x1, Pallas kernels, per_device(): pl.pallas_call(functools.partial(mixer_kernel, (rows, cols, users, heads,...  27.9 us
    unnamed x1, local copies, waits for them, and re-layouts  1.32 us

profile of v7, /device:TPU:24, one launch (start us, length us, event | category | flops | bytes accessed | tf_op | source)
XLA Modules:
  0.0 29.2 jit_solution(4446665387042635133)
XLA Ops:
  0.0 27.9 %mixer.1 = bf16[1024,1024]{1,0:T(8,128)(2,1)S(1)} custom-call(s32[2]{0:T(128)} %lengths_hbm.1, s32[2,1,512]{2,1,0:T(1,128)} %ids_hbm.1, s32[2,1,512]{2,1,0:T(1,128)} %masks_hbm.1, bf16[8,1024]{1,0:T(8,128)(2,1)} %bitcast.8, f32[4,1280]{1,0:T(4,128)} %taps_hbm.1, f32[1,8]{1,0:T(1,128)} %bitcast.10, f32[1,8]{1,0:T(1,128)} %bitcast.11, f32[1,1024]{1,0:T(1,128)} %bitcast.9, ...), custom_call_target="tpu_custom_call" | custom-call | tf_op jit(solution)/shard_map/mixer/pallas_call | solution.py:699
  27.9 1.3 %copy.15 = bf16[2,1,512,1024]{3,2,1,0:T(8,128)(2,1)} copy(bf16[2,1,512,1024]{3,2,1,0:T(8,128)(2,1)S(1)} %bitcast.7) | data formatting | bytes 4194304
